TPU v7x, 256 devices: a whole 4x4x8 slice. The times are simulated.
256 devices in a mesh: gx: 8 (over y, z_lo), gy: 4 (over z_hi), gz: 8 (over x, core).
Axes of the slice: x: 4, y: 4, z: 8 (z_hi: 4, z_lo: 2; z = z_hi * 2 + z_lo), core: 2. Of those that a mesh axis runs over, the one named last changes fastest.
Arguments:
- node_latent: bfloat16 [8, 4, 8, 512, 128], P('gx', 'gy', 'gz'), may hold values from -6 to 6
- ghost_latent: bfloat16 [8, 4, 8, 6, 64, 128], P('gx', 'gy', 'gz'), may hold values from -6 to 6
- edge_latent: bfloat16 [8, 4, 8, 2816, 128], P('gx', 'gy', 'gz'), may hold values from -6 to 6
- senders: int32 [8, 4, 8, 2816], P('gx', 'gy', 'gz'), may hold values from 0 to 895
- receivers: int32 [8, 4, 8, 2816], P('gx', 'gy', 'gz'), may hold values from 0 to 511, never falling along the last dimension, each value on 1 to 12 neighbouring positions
- export_rows: int32 [8, 4, 8, 6, 64], P('gx', 'gy', 'gz'), may hold values from 0 to 512, as said below
- node_cotangent: bfloat16 [8, 4, 8, 512, 128], P('gx', 'gy', 'gz'), may hold values from -6 to 6
- edge_cotangent: bfloat16 [8, 4, 8, 2816, 128], P('gx', 'gy', 'gz'), may hold values from -6 to 6
- w_edge_in: bfloat16 [384, 128], replicated, may hold values from -0.3125 to 0.3125
- w_edge_hidden: bfloat16 [2, 128, 128], replicated, may hold values from -0.5 to 0.5
- b_edge: float32 [3, 128], replicated, may hold values from -3 to 3
- gain_edge: float32 [128], replicated, may hold values from 0.1 to 1.9
- shift_edge: float32 [128], replicated, may hold values from -3 to 3
- w_node_in: bfloat16 [256, 128], replicated, may hold values from -0.375 to 0.375
- w_node_hidden: bfloat16 [2, 128, 128], replicated, may hold values from -0.5 to 0.5
- b_node: float32 [3, 128], replicated, may hold values from -3 to 3
- gain_node: float32 [128], replicated, may hold values from 0.1 to 1.9
Outputs:
- node_grad: float32 [8, 4, 8, 512, 128], P('gx', 'gy', 'gz')
- edge_grad: bfloat16 [8, 4, 8, 2816, 128], P('gx', 'gy', 'gz')
- grad_w_edge_in: float32 [384, 128], replicated
- grad_w_edge_hidden: float32 [2, 128, 128], replicated
- grad_b_edge: float32 [3, 128], replicated
- grad_gain_edge: float32 [128], replicated
- grad_shift_edge: float32 [128], replicated
- grad_w_node_in: float32 [256, 128], replicated
- grad_w_node_hidden: float32 [2, 128, 128], replicated
- grad_b_node: float32 [3, 128], replicated
- grad_gain_node: float32 [128], replicated
Inputs may be any that keep to these rules, and one draw needn't show every extreme that they name: `export_rows`: for each block and face the leading slots hold distinct owned rows of that block; the remaining slots hold 512, marking an empty slot.
All inputs are finite; a program needn't handle non-finite values.
Results may differ from a plain program's by a relative error of at most 0.02.
Values sent between devices are 32-bit elements; how exact they have to be, the bound alone decides.
A program may use at most 64 MiB of HBM per device.

v0:
```python
import jax
import jax.numpy as jnp
from jax import lax
from jax.sharding import PartitionSpec as P

EPSILON = 1e-05


def from_behind(x, axis, by):
    peers = lax.axis_size(axis)
    return lax.ppermute(x, axis, [(i, (i + by) % peers) for i in range(peers)])


def matmul(left, right):
    return jnp.dot(left, right, preferred_element_type=jnp.float32)


def contract_rows(left, right):
    return lax.dot_general(
        left, right, (((0,), (0,)), ((), ())), preferred_element_type=jnp.float32
    )


def silu_parts(preact):
    sigmoid = jax.nn.sigmoid(preact)
    return (preact * sigmoid, sigmoid * (1.0 + preact * (1.0 - sigmoid)))


def norm_parts(preact):
    centred = preact - jnp.mean(preact, -1, keepdims=True)
    inv_std = lax.rsqrt(jnp.mean(centred * centred, -1, keepdims=True) + EPSILON)
    return (centred * inv_std, inv_std)


def norm_back(grad_out, gain, normed, inv_std):
    scaled = grad_out * gain
    return inv_std * (
        scaled
        - jnp.mean(scaled, -1, keepdims=True)
        - normed * jnp.mean(scaled * normed, -1, keepdims=True)
    )


def mlp_forward(inputs, w_first, w_hidden, biases):
    first_pre = matmul(inputs, w_first) + biases[0]
    first_act, first_slope = silu_parts(first_pre)
    first_out = first_act.astype(jnp.bfloat16)
    second_pre = matmul(first_out, w_hidden[0]) + biases[1]
    second_act, second_slope = silu_parts(second_pre)
    second_out = second_act.astype(jnp.bfloat16)
    final_pre = matmul(second_out, w_hidden[1]) + biases[2]
    return ((first_out, second_out, first_slope, second_slope), final_pre)


def mlp_back_inputs(final_grad, saved, w_first, w_hidden):
    first_out, second_out, first_slope, second_slope = saved
    final_round = final_grad.astype(jnp.bfloat16)
    second_grad = matmul(final_round, w_hidden[1].T) * second_slope
    second_round = second_grad.astype(jnp.bfloat16)
    first_grad = matmul(second_round, w_hidden[0].T) * first_slope
    first_round = first_grad.astype(jnp.bfloat16)
    input_grad = matmul(first_round, w_first.T)
    bias_grad = jnp.stack([jnp.sum(first_grad, 0), jnp.sum(second_grad, 0), jnp.sum(final_grad, 0)])
    return ((first_round, second_round, final_round), bias_grad, input_grad)


def mlp_back_weights(inputs, saved, rounded):
    first_weight = contract_rows(inputs, rounded[0])
    hidden_weight = jnp.stack(
        [contract_rows(saved[0], rounded[1]), contract_rows(saved[1], rounded[2])]
    )
    return (first_weight, hidden_weight)


def forward_states(node_rows, ghost_rows, edge_rows, sender_ids, receiver_ids, params):
    node_count, feature_width = node_rows.shape
    full_rows = jnp.concatenate([node_rows, ghost_rows.reshape(-1, feature_width)], 0)
    edge_inputs = jnp.concatenate([edge_rows, full_rows[sender_ids], full_rows[receiver_ids]], 1)
    edge_stored_state, edge_pre = mlp_forward(edge_inputs, params[0], params[1], params[2])
    edge_normed, edge_inv = norm_parts(edge_pre)
    edge_new = (edge_normed * params[3] + params[4]).astype(jnp.bfloat16)
    aggregate = jax.ops.segment_sum(
        edge_new.astype(jnp.float32), receiver_ids, num_segments=node_count
    ).astype(jnp.bfloat16)
    node_input_rows = jnp.concatenate([node_rows, aggregate], 1)
    node_saved, node_pre = mlp_forward(node_input_rows, params[5], params[6], params[7])
    node_normed, node_inv = norm_parts(node_pre)
    return (
        (edge_inputs, edge_stored_state, edge_normed, edge_inv),
        (node_input_rows, node_saved, node_normed, node_inv),
    )


def node_backward(node_state, node_cot, params):
    node_input_rows, node_saved, node_normed, node_inv = node_state
    upstream = node_cot.astype(jnp.float32)
    gain_grad = jnp.sum(upstream * node_normed, 0)
    final_grad = norm_back(upstream, params[8], node_normed, node_inv)
    rounded, bias_grad, input_grad = mlp_back_inputs(final_grad, node_saved, params[5], params[6])
    first_weight, hidden_weight = mlp_back_weights(node_input_rows, node_saved, rounded)
    return (input_grad, (first_weight, hidden_weight, bias_grad, gain_grad))


def edge_backward_inputs(
    edge_state, edge_cot, agg_grad, sender_ids, receiver_ids, total_rows, params
):
    edge_inputs, edge_stored_state, edge_normed, edge_inv = edge_state
    feature_width = edge_cot.shape[1]
    edge_upstream = edge_cot.astype(jnp.float32)
    new_grad = edge_upstream + agg_grad[receiver_ids]
    gain_grad = jnp.sum(new_grad * edge_normed, 0)
    shift_grad = jnp.sum(new_grad, 0)
    final_grad = norm_back(new_grad, params[3], edge_normed, edge_inv)
    rounded, bias_grad, input_grad = mlp_back_inputs(
        final_grad, edge_stored_state, params[0], params[1]
    )
    edge_grad = (edge_upstream + input_grad[:, :feature_width]).astype(jnp.bfloat16)
    full_grad = jax.ops.segment_sum(
        input_grad[:, feature_width : 2 * feature_width], sender_ids, num_segments=total_rows
    )
    full_grad = full_grad + jax.ops.segment_sum(
        input_grad[:, 2 * feature_width :], receiver_ids, num_segments=total_rows
    )
    return (edge_grad, full_grad, rounded, (bias_grad, gain_grad, shift_grad))


def send_back(ghost_grad):
    returned = []
    for side_index in range(2):
        returned.append(from_behind(ghost_grad[side_index], "gx", 1 - 2 * side_index))
    for side_index in range(2):
        returned.append(from_behind(ghost_grad[2 + side_index], "gy", 1 - 2 * side_index))
    for side_index in range(2):
        returned.append(from_behind(ghost_grad[4 + side_index], "gz", 1 - 2 * side_index))
    return returned


def on_device(
    node_latent,
    ghost_latent,
    edge_latent,
    senders,
    receivers,
    export_rows,
    node_cotangent,
    edge_cotangent,
    w_edge_in,
    w_edge_hidden,
    b_edge,
    gain_edge,
    shift_edge,
    w_node_in,
    w_node_hidden,
    b_node,
    gain_node,
):
    params = (
        w_edge_in,
        w_edge_hidden,
        b_edge,
        gain_edge,
        shift_edge,
        w_node_in,
        w_node_hidden,
        b_node,
        gain_node,
    )
    node_count = node_latent.shape[3]
    feature_width = node_latent.shape[4]
    node_rows = node_latent.reshape(node_count, feature_width)
    ghost_rows = ghost_latent.reshape(ghost_latent.shape[3:])
    edge_rows = edge_latent.reshape(edge_latent.shape[3:])
    edge_count = edge_rows.shape[0]
    sender_ids = senders.reshape(edge_count)
    receiver_ids = receivers.reshape(edge_count)
    face_rows = export_rows.reshape(export_rows.shape[3:])
    node_cot = node_cotangent.reshape(node_count, feature_width)
    edge_cot = edge_cotangent.reshape(edge_count, feature_width)
    devices = lax.axis_size("gx") * lax.axis_size("gy") * lax.axis_size("gz")
    edge_scale = float(edge_count * devices) ** (-0.5)
    node_scale = float(node_count * devices) ** (-0.5)
    total_rows = node_count + ghost_rows.shape[0] * ghost_rows.shape[1]
    edge_state, node_state = forward_states(
        node_rows, ghost_rows, edge_rows, sender_ids, receiver_ids, params
    )
    node_input_grad, node_weights = node_backward(node_state, node_cot, params)
    edge_grad, full_grad, rounded, edge_small = edge_backward_inputs(
        edge_state,
        edge_cot,
        node_input_grad[:, feature_width:],
        sender_ids,
        receiver_ids,
        total_rows,
        params,
    )
    ghost_grad = full_grad[node_count:].reshape(ghost_rows.shape)
    first_weight, hidden_weight = mlp_back_weights(edge_state[0], edge_state[1], rounded)
    returned = send_back(ghost_grad)
    edge_weights = (first_weight, hidden_weight) + edge_small
    summed = tuple(lax.psum(edge_weights + node_weights, ("gx", "gy", "gz")))
    edge_weights = summed[:5]
    node_weights = summed[5:]
    local_grad = (
        node_cot.astype(jnp.float32) + node_input_grad[:, :feature_width] + full_grad[:node_count]
    )
    for face_index in range(6):
        local_grad = local_grad.at[face_rows[face_index]].add(returned[face_index], mode="drop")
    node_grad = local_grad.reshape(node_latent.shape)
    edge_out = edge_grad.reshape(edge_latent.shape)
    return (
        node_grad,
        edge_out,
        edge_weights[0] * edge_scale,
        edge_weights[1] * edge_scale,
        edge_weights[2] * edge_scale,
        edge_weights[3] * edge_scale,
        edge_weights[4] * edge_scale,
        node_weights[0] * node_scale,
        node_weights[1] * node_scale,
        node_weights[2] * node_scale,
        node_weights[3] * node_scale,
    )


def solution(mesh):
    in_specs = (
        P("gx", "gy", "gz", None, None),
        P("gx", "gy", "gz", None, None, None),
        P("gx", "gy", "gz", None, None),
        P("gx", "gy", "gz", None),
        P("gx", "gy", "gz", None),
        P("gx", "gy", "gz", None, None),
        P("gx", "gy", "gz", None, None),
        P("gx", "gy", "gz", None, None),
        P(),
        P(),
        P(),
        P(),
        P(),
        P(),
        P(),
        P(),
        P(),
    )
    out_specs = (
        P("gx", "gy", "gz", None, None),
        P("gx", "gy", "gz", None, None),
        P(),
        P(),
        P(),
        P(),
        P(),
        P(),
        P(),
        P(),
        P(),
    )
    return jax.shard_map(
        on_device, mesh=mesh, in_specs=in_specs, out_specs=out_specs, check_vma=False
    )
```

profile of v0, /device:TPU:1, one launch (start us, length us, event | category | flops | bytes accessed | tf_op | source)
XLA Modules:
  0.0 396.3 jit_solution(4633995178158212328)
XLA Ops:
  7.2 0.7 fusion.51
  8.0 1.3 reduce.3
  9.3 0.7 reduce
  10.1 0.8 fusion.53
  10.8 0.8 slice_bitcast_fusion.5
  11.6 0.8 slice_bitcast_fusion
  12.4 1.0 copy.37
  13.5 1.0 pad_maximum_fusion.4
  14.5 5.6 %gather_fusion.1 = bf16[2816,128]{1,0:T(8,128)(2,1)S(1)} fusion(bf16[896,128]{1,0:T(8,128)(2,1)S(1)} %pad_maximum_fusion.4, s32[3072]{0:T(1024)S(1)} %get-tuple-element.88), kind=kCustom, calls=%fused_computation.1 | custom fusion | bytes 1453056 | tf_op jit(solution)/shard_map/gather | solution.py:78
  20.1 5.6 %gather_fusion = bf16[2816,128]{1,0:T(8,128)(2,1)S(1)} fusion(bf16[896,128]{1,0:T(8,128)(2,1)S(1)} %pad_maximum_fusion.4, s32[3072]{0:T(1024)S(1)} %pad_clamp_fusion.2), kind=kCustom, calls=%fused_computation | custom fusion | bytes 1453056 | tf_op jit(solution)/shard_map/gather | solution.py:78
  25.7 1.1 copy.40
  26.9 1.9 convolution_add_fusion.2
  29.3 0.6 copy-done.47
  29.9 0.6 fusion.71
  32.0 1.6 copy.38
  33.5 19.6 %scatter_custom_fusion = f32[512,128]{1,0:T(8,128)S(1)} fusion(s32[2816]{0:T(1024)S(1)} %reduce, f32[2816,128]{1,0:T(8,128)} %copy.38, f32[]{:T(128)} %constant.9.clone.1), kind=kCustom, calls=%fused_computation.79 | custom fusion | flops 360448 | bytes 262656 | tf_op jit(solution)/shard_map/scatter-add | solution.py:82
  54.3 0.9 fusion.75
  55.1 0.8 fusion.76
  56.1 0.7 fusion.69
  56.9 5.9 %gather_fusion.2 = f32[2816,128]{1,0:T(8,128)} fusion(f32[512,128]{1,0:T(8,128)S(1)} %get-tuple-element.54, s32[3072]{0:T(1024)S(1)} %get-tuple-element.87), kind=kCustom, calls=%fused_computation.2 | custom fusion | bytes 2894848 | tf_op jit(solution)/shard_map/gather | solution.py:110
  62.8 1.8 copy.41
  64.6 3.1 multiply_reduce_fusion
  67.8 0.7 fusion.68
  69.2 1.3 fusion.73
  70.5 1.3 fusion.74
  71.8 2.7 fusion.12
  74.5 19.4 %scatter_custom_fusion.2 = f32[896,128]{1,0:T(8,128)S(1)} fusion(s32[2816]{0:T(1024)} %copy-done.23, f32[2816,384]{1,0:T(8,128)} %fusion.12, f32[]{:T(128)} %constant.9.clone.1), kind=kCustom, calls=%fused_computation.21 | custom fusion | flops 360448 | bytes 1901056 | tf_op jit(solution)/shard_map/scatter-add | solution.py:121
  94.1 15.9 %scatter_custom_fusion.1 = f32[896,128]{1,0:T(8,128)S(1)} fusion(s32[2816]{0:T(1024)} %reduce.3, f32[2816,384]{1,0:T(8,128)} %fusion.12, f32[]{:T(128)} %constant.9.clone.1), kind=kCustom, calls=%fused_computation.23 | custom fusion | flops 360448 | bytes 1901056 | tf_op jit(solution)/shard_map/scatter-add | solution.py:118
  110.3 0.8 fusion.70
  111.1 3.2 collective-permute-start.5
  114.3 5.4 %collective-permute-start.3 = (f32[64,128]{0,1:T(8,128)}, f32[64,128]{0,1:T(8,128)}, u32[]{:S(2)}, u32[]{:S(2)}) collective-permute-start(f32[64,128]{0,1:T(8,128)} %get-tuple-element.58), channel_id=1, source_target_pairs={{0,24},{8,0},{16,8},{24,16},{1,25},{9,1},{17,9},{25,17},{2,26},{10... | collective-permute-start | bytes 98312 | tf_op jit(solution)/shard_map/ppermute | solution.py:11
  119.8 0.8 collective-permute-start
  121.2 0.9 fusion.25
  122.1 0.7 convolution_bitcast_fusion
  122.8 0.7 copy-done.49
  123.7 0.6 convolution_bitcast_fusion.1
  125.2 1.5 fusion.5
  126.7 0.7 pad_maximum_fusion.8
  127.3 0.7 pad_maximum_fusion.7
  128.0 0.7 copy-done.28
  129.0 0.8 copy.53
  129.8 1.6 copy.54
  131.4 1.6 fusion.7
  133.3 80.1 %all-reduce = (f32[3,128]{1,0:T(4,128)S(1)}, f32[128]{0:T(128)S(1)}, f32[128]{0:T(128)S(1)}, f32[3,128]{1,0:T(4,128)S(1)}, f32[128]{0:T(128)S(1)}) all-reduce(f32[3,128]{1,0:T(4,128)S(1)} %pad_maximum_fusion.9, f32[128]{0:T(128)S(1)} %copy-done.31, f32[128]{0:T(128)S(1)} %copy-done.32, ...), channel_id=1, replica_groups=mesh['gx'=8,'gy'=4,'gz'=8] {'gx','gy','gz'}, use_global_device_ids=true, to_apply=%region_22.0 | all-reduce | flops 1152 | bytes 9216 | tf_op jit(solution)/shard_map/psum | solution.py:200
  213.4 0.6 broadcast_multiply_fusion.8
  214.5 0.6 broadcast_multiply_fusion.7
  215.6 0.6 collective-permute-start.1
  216.7 1.1 copy.52
  218.0 0.9 copy.45
  218.9 1.0 scatter_fusion
  220.0 1.0 scatter_fusion.1
  221.1 0.9 copy.47
  222.0 1.0 scatter_fusion.2
  223.0 0.9 copy.48
  223.9 1.0 scatter_fusion.3
  225.0 0.9 copy.49
  225.9 1.0 scatter_fusion.4
  227.0 0.9 copy.50
  227.9 1.0 scatter_fusion.5
  228.9 154.2 %all-reduce.4.cloned.1.call-done = (f32[384,128]{1,0:T(8,128)}, f32[2,128,128]{2,1,0:T(8,128)}, f32[256,128]{1,0:T(8,128)}, f32[2,128,128]{2,1,0:T(8,128)}) async-done(((f32[384,128]{1,0:T(8,128)}, f32[2,128,128]{2,1,0:T(8,128)}, f32[256,128]{1,0:T(8,128)}, f32[2,128,128]{2,1,0:T(8,128)}), (f32[384,128]{1,0:T(8,128)}, f32[2,128,128]{2,1,0:T(8,128)}, f32[256,128]{1,0:T(8,128)}, ...) | async-done | bytes 589840 | tf_op jit(solution)/shard_map/psum | solution.py:200
  383.1 1.6 broadcast_multiply_fusion
  384.8 1.6 broadcast_multiply_fusion.3
  386.3 1.6 broadcast_multiply_fusion.2
  387.9 1.6 broadcast_multiply_fusion.1
  (153 shorter events, 8.5 us)
Async XLA Ops:
  7.2 19.7 %copy-start = (bf16[384,128]{1,0:T(8,128)(2,1)S(1)}, bf16[384,128]{1,0:T(8,128)(2,1)}, u32[]{:S(2)}) copy-start(bf16[384,128]{1,0:T(8,128)(2,1)} %param.25) | copy-start | bytes 294916
  7.2 375.9 %all-reduce.4.cloned.1.call-start = ((), (), s32[]{:S(2)}) async-start(), calls=%async_computation | async-start | bytes 1179648 | tf_op jit(solution)/shard_map/psum | solution.py:200
  10.1 23.5 %copy-start.23 = (s32[2816]{0:T(1024)}, s32[2816]{0:T(1024)S(1)}, u32[]{:S(2)}) copy-start(s32[2816]{0:T(1024)S(1)} %reduce) | copy-start | bytes 33796
  20.1 6.8 %copy-start.9 = (bf16[2816,128]{1,0:T(8,128)(2,1)}, bf16[2816,128]{1,0:T(8,128)(2,1)S(1)}, u32[]{:S(2)}) copy-start(bf16[2816,128]{1,0:T(8,128)(2,1)S(1)} %gather_fusion.1) | copy-start | bytes 2162692
  20.1 5.6 %copy-start.8 = (bf16[1,1,1,2816,128]{4,3,2,1,0:T(8,128)(2,1)S(1)}, bf16[1,1,1,2816,128]{4,3,2,1,0:T(8,128)(2,1)}, u32[]{:S(2)}) copy-start(bf16[1,1,1,2816,128]{4,3,2,1,0:T(8,128)(2,1)} %param.24) | copy-start | bytes 2162692
  25.7 3.0 copy-start.11
  26.9 1.9 copy-start.41
  28.7 1.1 copy-start.47
  29.9 1.1 copy-start.50
  31.0 0.7 copy-start.26
  31.0 0.7 copy-start.37
  32.0 21.2 %copy-start.13 = (bf16[1,1,1,512,128]{4,3,2,1,0:T(8,128)(2,1)S(1)}, bf16[1,1,1,512,128]{4,3,2,1,0:T(8,128)(2,1)}, u32[]{:S(2)}) copy-start(bf16[1,1,1,512,128]{4,3,2,1,0:T(8,128)(2,1)} %param.17) | copy-start | bytes 393220
  32.0 21.2 %copy-start.18 = (bf16[256,128]{1,0:T(8,128)(2,1)S(1)}, bf16[256,128]{1,0:T(8,128)(2,1)}, u32[]{:S(2)}) copy-start(bf16[256,128]{1,0:T(8,128)(2,1)} %param.30) | copy-start | bytes 196612
  32.0 21.5 %copy-start.39 = (bf16[2,128,128]{2,1,0:T(8,128)(2,1)S(1)}, bf16[2,128,128]{2,1,0:T(8,128)(2,1)}, u32[]{:S(2)}) copy-start(bf16[2,128,128]{2,1,0:T(8,128)(2,1)} %param.31) | copy-start | bytes 196612
  33.5 20.1 %copy-start.40 = (bf16[2,128,128]{2,1,0:T(8,128)(2,1)S(1)}, bf16[2,128,128]{2,1,0:T(8,128)(2,1)}, u32[]{:S(2)}) copy-start(bf16[2,128,128]{2,1,0:T(8,128)(2,1)} %param.31) | copy-start | bytes 196612
  53.1 0.8 copy-start.14
  53.4 1.7 copy-start.16
  53.4 0.7 copy-start.29
  53.6 1.5 copy-start.43
  54.2 1.6 copy-start.24
  54.3 1.6 copy-start.19
  55.1 1.7 copy-start.45
  55.9 1.0 copy-start.20
  62.8 1.8 copy-start.27
  64.6 3.1 copy-start.2
  67.8 0.8 copy-start.42
  67.8 1.4 copy-start.51
  68.5 1.9 copy-start.6
  69.2 1.4 copy-start.48
  70.4 1.3 copy-start.53
  110.0 10.6 %copy-start.25 = (f32[512]{0:T(512)S(1)}, f32[512]{0:T(512)}, u32[]{:S(2)}) copy-start(f32[512]{0:T(512)} %copy-done.24) | copy-start | bytes 6148
  110.0 10.6 %copy-start.30 = (f32[128]{0:T(128)S(1)}, f32[128]{0:T(128)}, u32[]{:S(2)}) copy-start(f32[128]{0:T(128)} %param.33) | copy-start | bytes 1540
  110.2 10.4 %copy-start.44 = (f32[512,128]{1,0:T(8,128)S(1)}, f32[512,128]{1,0:T(8,128)}, u32[]{:S(2)}) copy-start(f32[512,128]{1,0:T(8,128)} %copy-done.43) | copy-start | bytes 786436
  110.3 10.6 %copy-start.17 = (f32[512,128]{1,0:T(8,128)S(1)}, f32[512,128]{1,0:T(8,128)}, u32[]{:S(2)}) copy-start(f32[512,128]{1,0:T(8,128)} %copy-done.16) | copy-start | bytes 786436
  110.3 10.6 %copy-start.46 = (bf16[512,128]{1,0:T(8,128)(2,1)S(1)}, bf16[512,128]{1,0:T(8,128)(2,1)}, u32[]{:S(2)}) copy-start(bf16[512,128]{1,0:T(8,128)(2,1)} %copy-done.45) | copy-start | bytes 393220
  111.1 115.8 %collective-permute-start.5 = (f32[64,128]{0,1:T(8,128)}, f32[64,128]{0,1:T(8,128)}, u32[]{:S(2)}, u32[]{:S(2)}) collective-permute-start(f32[64,128]{0,1:T(8,128)} %get-tuple-element.56), channel_id=1, source_target_pairs={{0,7},{1,0},{2,1},{3,2},{4,3},{5,4},{6,5},{7,6},{8,15},{9,8},{10,9... | collective-permute-start | bytes 98312 | tf_op jit(solution)/shard_map/ppermute | solution.py:11
  114.3 110.7 %collective-permute-start.4 = (f32[64,128]{0,1:T(8,128)}, f32[64,128]{0,1:T(8,128)}, u32[]{:S(2)}, u32[]{:S(2)}) collective-permute-start(f32[64,128]{0,1:T(8,128)} %get-tuple-element.57), channel_id=1, source_target_pairs={{0,1},{1,2},{2,3},{3,4},{4,5},{5,6},{6,7},{7,0},{8,9},{9,10},{10,1... | collective-permute-start | bytes 98312 | tf_op jit(solution)/shard_map/ppermute | solution.py:11
  114.3 108.7 %collective-permute-start.3 = (f32[64,128]{0,1:T(8,128)}, f32[64,128]{0,1:T(8,128)}, u32[]{:S(2)}, u32[]{:S(2)}) collective-permute-start(f32[64,128]{0,1:T(8,128)} %get-tuple-element.58), channel_id=1, source_target_pairs={{0,24},{8,0},{16,8},{24,16},{1,25},{9,1},{17,9},{25,17},{2,26},{10... | collective-permute-start | bytes 98312 | tf_op jit(solution)/shard_map/ppermute | solution.py:11
  119.8 101.3 %collective-permute-start.2 = (f32[64,128]{0,1:T(8,128)}, f32[64,128]{0,1:T(8,128)}, u32[]{:S(2)}, u32[]{:S(2)}) collective-permute-start(f32[64,128]{0,1:T(8,128)} %get-tuple-element.59), channel_id=1, source_target_pairs={{0,8},{8,16},{16,24},{24,0},{1,9},{9,17},{17,25},{25,1},{2,10},{10... | collective-permute-start | bytes 98312 | tf_op jit(solution)/shard_map/ppermute | solution.py:11
  119.8 1.4 copy-start.15
  119.8 1.4 copy-start.21
  119.8 2.4 copy-start.7
  119.8 2.4 copy-start.52
  119.8 95.8 %collective-permute-start = (f32[64,128]{0,1:T(8,128)}, f32[64,128]{0,1:T(8,128)}, u32[]{:S(2)}, u32[]{:S(2)}) collective-permute-start(f32[64,128]{0,1:T(8,128)} %get-tuple-element.61), channel_id=1, source_target_pairs={{0,32},{32,64},{64,96},{96,128},{128,160},{160,192},{192,224},{224... | collective-permute-start | bytes 98312 | tf_op jit(solution)/shard_map/ppermute | solution.py:11
  122.1 1.4 copy-start.49
  122.1 1.5 copy-start.54
  123.7 1.1 copy-start.10
  123.7 1.3 copy-start.12
  123.7 1.5 copy-start.38
  128.0 0.7 copy-start.28
  128.0 1.0 copy-start.5
  128.0 1.8 slice-start
  129.8 1.6 copy-start.3
  131.4 1.7 copy-start.4
  131.4 1.9 copy-start.35
  131.4 1.9 copy-start.36
  131.4 1.9 copy-start.33
  131.4 1.9 copy-start.34
  131.4 1.9 copy-start.31
  131.4 1.9 copy-start.32
  131.4 84.2 %copy-start.22 = (f32[64,128]{0,1:T(8,128)S(1)}, f32[64,128]{0,1:T(8,128)}, u32[]{:S(2)}) copy-start(f32[64,128]{0,1:T(8,128)} %get-tuple-element.60) | copy-start | bytes 98308
  215.6 4.3 %collective-permute-start.1 = (f32[64,128]{0,1:T(8,128)S(1)}, f32[64,128]{0,1:T(8,128)S(1)}, u32[]{:S(2)}, u32[]{:S(2)}) collective-permute-start(f32[64,128]{0,1:T(8,128)S(1)} %copy-done.22), channel_id=1, source_target_pairs={{0,224},{32,0},{64,32},{96,64},{128,96},{160,128},{192,160},{224,1... | collective-permute-start | bytes 98312 | tf_op jit(solution)/shard_map/ppermute | solution.py:11
  228.9 160.6 %copy-start.1 = (f32[512,128]{1,0:T(8,128)}, f32[512,128]{1,0:T(8,128)S(1)}, u32[]{:S(2)}) copy-start(f32[512,128]{1,0:T(8,128)S(1)} %scatter_fusion.5) | copy-start | bytes 786436
Sparse Core Ops, SparseCore 0:
  128.1 254.9 all-reduce.3
where the time goes:
time: 397 us; the launch traced here: 396 us
  waiting for transfers between devices  154 us (39%)
  other arithmetic  82.4 us (21%)
  blocking collectives  80.1 us (20%)
  local copies, waits for them, and re-layouts  39.8 us (10%)
  matrix products  14.9 us (4%)
  between operations  14.8 us (4%)
  starting transfers between devices  10.1 us (3%)
    psum x1, waiting for transfers between devices, on_device(): summed = tuple(lax.psum(edge_weights + node_weights, ('gx', 'gy', 'gz')))  154 us
    psum x1, blocking collectives, on_device(): summed = tuple(lax.psum(edge_weights + node_weights, ('gx', 'gy', 'gz')))  80.1 us
    scatter-add x1, other arithmetic, forward_states(): jax.ops.segment_sum(edge_new.astype(jnp.float32), receiver_ids, num_segme...  19.6 us
    scatter-add x1, other arithmetic, edge_backward_inputs(): jax.ops.segment_sum(input_grad[:, 2 * feature_width:], receiver_ids, num_...  19.4 us
    scatter-add x1, other arithmetic, edge_backward_inputs(): jax.ops.segment_sum(input_grad[:, feature_width:2 * feature_width], sende...  15.9 us
    unnamed x115, local copies, waits for them, and re-layouts  11 us
    dot_general x12, matrix products, matmul(): return jnp.dot(left, right, preferred_element_type=jnp.float32)  10.7 us
    ppermute x6, starting transfers between devices, from_behind(): return lax.ppermute(x, axis, [(i, (i + by) % peers) for i in range(peers)])  10 us
  transfers between devices with their start and end apart: 7, of which 1 were waited for; matrix products, arithmetic and copies ran while one was open for 6% of the time, Pallas kernels for 0%

commit v1 on v0

v1 whole, which is shorter than its diff:
```python
import functools

import jax
import jax.numpy as jnp
from jax import lax
from jax.experimental import pallas as pl
from jax.experimental.pallas import tpu as pltpu
from jax.sharding import PartitionSpec as P

EPSILON = 1e-05
MESH = pl.DeviceIdType.MESH
BF = jnp.bfloat16
F32 = jnp.float32
D = 128
NODES = 512
FACES = 6
SLOTS = 64
FULL = NODES + FACES * SLOTS
EDGES = 2816
CH = 256
CHUNKS = EDGES // CH
SEND_TILES = FULL // D
RECV_TILES = NODES // D
TILES = SEND_TILES + RECV_TILES
PIECES = 32
PIECE = 40
ROW_EW1 = 0
ROW_EWH = 384
ROW_ESM = 640
ROW_NW1 = 648
ROW_NWH = 904
ROW_NSM = 1160
ROWS = PIECES * PIECE


def mm(a, b):
    return jnp.dot(a, b, preferred_element_type=F32)


def mm_tn(a, b):
    return lax.dot_general(a, b, (((0,), (0,)), ((), ())), preferred_element_type=F32)


def transposed(w):
    return w.astype(F32).T.astype(BF)


def silu_parts(p):
    s = 0.5 * jnp.tanh(0.5 * p) + 0.5
    z = p * s
    return z, s + z * (1.0 - s)


def norm_parts(p):
    c = p - jnp.mean(p, -1, keepdims=True)
    inv = lax.rsqrt(jnp.mean(c * c, -1, keepdims=True) + EPSILON)
    return c * inv, inv


def norm_back(u, gain, n, inv):
    t = u * gain
    return inv * (t - jnp.mean(t, -1, keepdims=True) - n * jnp.mean(t * n, -1, keepdims=True))


def fold(x):
    return jnp.sum(x.reshape(x.shape[0] // 8, 8, x.shape[1]), 0)


def row_sum(x):
    return jnp.sum(fold(x), 0, keepdims=True)


def column_digits(ids_row):
    lo, hi = [], []
    for j in range(ids_row.shape[1] // D):
        t = jnp.broadcast_to(ids_row[:, j * D : (j + 1) * D], (D, D)).T
        lo.append((t & (D - 1)).astype(F32).astype(BF))
        hi.append((t >> 7).astype(F32).astype(BF))
    return jnp.concatenate(lo, 0), jnp.concatenate(hi, 0)


def one_hot_columns(lo, hi, tiles):
    lane = lax.broadcasted_iota(jnp.int32, lo.shape, 1).astype(F32).astype(BF)
    zero = jnp.zeros(lo.shape, BF)
    base = jnp.where(lo == lane, jnp.ones(lo.shape, BF), zero)
    return [jnp.where(hi == BF(k), base, zero) for k in range(tiles)]


def one_hot_rows(ids_row, tiles):
    n = ids_row.shape[1]
    lo = jnp.broadcast_to((ids_row & (D - 1)).astype(F32), (D, n)).astype(BF)
    hi = jnp.broadcast_to((ids_row >> 7).astype(F32), (D, n)).astype(BF)
    row = lax.broadcasted_iota(jnp.int32, (D, n), 0).astype(F32).astype(BF)
    zero = jnp.zeros((D, n), BF)
    base = jnp.where(lo == row, jnp.ones((D, n), BF), zero)
    return [jnp.where(hi == BF(k), base, zero) for k in range(tiles)]


def compute_kernel(
    scales,
    node_ref, ghost_ref, edge_ref, send_ref, recv_ref, ncot_ref, ecot_ref,
    ew1_ref, ewh_ref, eb_ref, eg_ref, es_ref, nw1_ref, nwh_ref, nb_ref, ng_ref,
    local_ref, ghost_out_ref, edge_out_ref, pack_ref,
    table, z1, z2, sl1, sl2, nrm, inv, rlo, rhi, agg, acc, w3t, w2t, w1t, aggb, small,
):
    edge_scale, node_scale = scales
    node = node_ref[0, 0, 0]
    ghosts = ghost_ref[0, 0, 0].reshape(FACES * SLOTS, D)
    full = jnp.concatenate([node, ghosts], 0)
    table[0:FULL] = mm(full, ew1_ref[D : 2 * D]).astype(BF)
    table[FULL : FULL + NODES] = mm(node, ew1_ref[2 * D : 3 * D]).astype(BF)
    table[FULL + NODES :] = ew1_ref[0:D]
    w3t[...] = transposed(ewh_ref[1])
    w2t[...] = transposed(ewh_ref[0])
    w1t[...] = transposed(ew1_ref[0:D])
    agg[...] = jnp.zeros_like(agg)
    acc[...] = jnp.zeros_like(acc)
    small[...] = jnp.zeros_like(small)
    pack_ref[...] = jnp.zeros_like(pack_ref)
    egain = eg_ref[...].reshape(1, D)
    eshift = es_ref[...].reshape(1, D)

    def forward(i, carry):
        off = pl.multiple_of(i * CH, CH)
        rows = pl.ds(off, CH)
        s_row = send_ref[0, 0, :, rows]
        r_row = recv_ref[0, 0, :, rows]
        slo, shi = column_digits(s_row)
        lo, hi = column_digits(r_row)
        rlo[rows] = lo
        rhi[rows] = hi
        hot = one_hot_columns(slo, shi, SEND_TILES) + one_hot_columns(lo, hi, RECV_TILES)
        lhs = jnp.concatenate(hot + [edge_ref[0, 0, 0, rows]], 1)
        p1 = mm(lhs, table[...]) + eb_ref[0:1]
        a1, d1 = silu_parts(p1)
        b1 = a1.astype(BF)
        z1[rows] = b1
        sl1[rows] = d1
        p2 = mm(b1, ewh_ref[0]) + eb_ref[1:2]
        a2, d2 = silu_parts(p2)
        b2 = a2.astype(BF)
        z2[rows] = b2
        sl2[rows] = d2
        q = mm(b2, ewh_ref[1]) + eb_ref[2:3]
        n, iv = norm_parts(q)
        nrm[rows] = n
        inv[rows] = jnp.broadcast_to(iv, (CH, D))
        new = (n * egain + eshift).astype(BF)
        hot_t = jnp.concatenate(one_hot_rows(r_row, RECV_TILES), 0)
        agg[...] += mm(hot_t, new)
        return carry

    lax.fori_loop(0, CHUNKS, forward, 0)

    ngain = ng_ref[...].reshape(1, D)
    node_in = jnp.concatenate([node, agg[...].astype(BF)], 1)
    a1, d1 = silu_parts(mm(node_in, nw1_ref[...]) + nb_ref[0:1])
    b1 = a1.astype(BF)
    a2, d2 = silu_parts(mm(b1, nwh_ref[0]) + nb_ref[1:2])
    b2 = a2.astype(BF)
    n, iv = norm_parts(mm(b2, nwh_ref[1]) + nb_ref[2:3])
    u = ncot_ref[0, 0, 0].astype(F32)
    g3 = norm_back(u, ngain, n, iv)
    h3 = g3.astype(BF)
    g2 = mm(h3, transposed(nwh_ref[1])) * d2
    h2 = g2.astype(BF)
    g1 = mm(h2, transposed(nwh_ref[0])) * d1
    h1 = g1.astype(BF)
    local_ref[...] = u + mm(h1, transposed(nw1_ref[0:D]))
    aggb[...] = mm(h1, transposed(nw1_ref[D : 2 * D])).astype(BF)
    pack_ref[ROW_NW1 : ROW_NW1 + 2 * D] = mm_tn(node_in, h1) * node_scale
    pack_ref[ROW_NWH : ROW_NWH + D] = mm_tn(b1, h2) * node_scale
    pack_ref[ROW_NWH + D : ROW_NWH + 2 * D] = mm_tn(b2, h3) * node_scale
    pack_ref[ROW_NSM : ROW_NSM + 4] = node_scale * jnp.concatenate(
        [row_sum(g1), row_sum(g2), row_sum(g3), row_sum(u * n)], 0
    )

    def backward(i, carry):
        off = pl.multiple_of(i * CH, CH)
        rows = pl.ds(off, CH)
        s_row = send_ref[0, 0, :, rows]
        r_row = recv_ref[0, 0, :, rows]
        hot = jnp.concatenate(one_hot_columns(rlo[rows], rhi[rows], RECV_TILES), 1)
        cot = ecot_ref[0, 0, 0, rows].astype(F32)
        u = cot + mm(hot, aggb[...])
        n = nrm[rows]
        g3 = norm_back(u, egain, n, inv[rows])
        h3 = g3.astype(BF)
        g2 = mm(h3, w3t[...]) * sl2[rows]
        h2 = g2.astype(BF)
        g1 = mm(h2, w2t[...]) * sl1[rows]
        h1 = g1.astype(BF)
        edge_out_ref[0, 0, 0, rows] = (cot + mm(h1, w1t[...])).astype(BF)
        pack_ref[ROW_EW1 : ROW_EW1 + D] += mm_tn(edge_ref[0, 0, 0, rows], h1)
        pack_ref[ROW_EWH : ROW_EWH + D] += mm_tn(z1[rows], h2)
        pack_ref[ROW_EWH + D : ROW_EWH + 2 * D] += mm_tn(z2[rows], h3)
        hot_t = jnp.concatenate(one_hot_rows(s_row, SEND_TILES) + one_hot_rows(r_row, RECV_TILES), 0)
        acc[...] += mm(hot_t, h1)
        small[0] += fold(g1)
        small[1] += fold(g2)
        small[2] += fold(g3)
        small[3] += fold(u * n)
        small[4] += fold(u)
        return carry

    lax.fori_loop(0, CHUNKS, backward, 0)

    sums = acc[0:FULL].astype(BF)
    sums_r = acc[FULL : FULL + NODES].astype(BF)
    back = mm(sums, transposed(ew1_ref[D : 2 * D]))
    local_ref[...] += back[0:NODES] + mm(sums_r, transposed(ew1_ref[2 * D : 3 * D]))
    ghost_out_ref[...] = back[NODES:].reshape(FACES, SLOTS, D)
    pack_ref[ROW_EW1 : ROW_EW1 + D] = pack_ref[ROW_EW1 : ROW_EW1 + D] * edge_scale
    pack_ref[ROW_EW1 + D : ROW_EW1 + 2 * D] = mm_tn(full, sums) * edge_scale
    pack_ref[ROW_EW1 + 2 * D : ROW_EW1 + 3 * D] = mm_tn(node, sums_r) * edge_scale
    pack_ref[ROW_EWH : ROW_EWH + 2 * D] = pack_ref[ROW_EWH : ROW_EWH + 2 * D] * edge_scale
    pack_ref[ROW_ESM : ROW_ESM + 5] = edge_scale * jnp.concatenate(
        [jnp.sum(small[j], 0, keepdims=True) for j in range(5)], 0
    )


VMEM = pl.BlockSpec(memory_space=pltpu.VMEM)


def local_compute(args, scales):
    return pl.pallas_call(
        functools.partial(compute_kernel, scales),
        out_shape=(
            jax.ShapeDtypeStruct((NODES, D), F32),
            jax.ShapeDtypeStruct((FACES, SLOTS, D), F32),
            jax.ShapeDtypeStruct((1, 1, 1, EDGES, D), BF),
            jax.ShapeDtypeStruct((ROWS, D), F32),
        ),
        in_specs=[VMEM] * len(args),
        out_specs=(VMEM,) * 4,
        scratch_shapes=[
            pltpu.VMEM((FULL + NODES + D, D), BF),
            pltpu.VMEM((EDGES, D), BF),
            pltpu.VMEM((EDGES, D), BF),
            pltpu.VMEM((EDGES, D), F32),
            pltpu.VMEM((EDGES, D), F32),
            pltpu.VMEM((EDGES, D), F32),
            pltpu.VMEM((EDGES, D), F32),
            pltpu.VMEM((EDGES, D), BF),
            pltpu.VMEM((EDGES, D), BF),
            pltpu.VMEM((NODES, D), F32),
            pltpu.VMEM((FULL + NODES, D), F32),
            pltpu.VMEM((D, D), BF),
            pltpu.VMEM((D, D), BF),
            pltpu.VMEM((D, D), BF),
            pltpu.VMEM((NODES, D), BF),
            pltpu.VMEM((5, 8, D), F32),
        ],
        compiler_params=pltpu.CompilerParams(vmem_limit_bytes=48 * 2**20),
        cost_estimate=pl.CostEstimate(flops=6_000_000_000, bytes_accessed=6_000_000, transcendentals=800_000),
    )(*args)


def comm_kernel(
    pack_ref, ghost_ref, local_ref, rows_ref,
    out_ref, node_ref,
    pair_buf, half, plane_buf, zbuf, fin, gbuf,
    pair_s, pair_r, plane_s, plane_r, z_s, z_r, ag_s, ag_r, back_s, back_r, g_s, g_r,
):
    gx, gy, gz = lax.axis_index("gx"), lax.axis_index("gy"), lax.axis_index("gz")
    y, zl = gx // 2, gx % 2
    x, c = gz // 2, gz % 2
    z = gy * 2 + zl
    plane = x * 4 + y
    sibling = (gx, gy, gz + 1 - 2 * c)

    def plane_peer(d):
        px, py = (x + d // 4) % 4, (y + d % 4) % 4
        return px * 4 + py, (py * 2 + zl, gy, px * 2 + c)

    def z_peer(d):
        pz = (z + d) % 8
        return (y * 2 + pz % 2, pz // 2, gz)

    ghost_to = []
    for f in range(FACES):
        step = 1 if f % 2 == 0 else -1
        ghost_to.append((
            ((gx + step + 8) % 8, gy, gz),
            (gx, (gy + step + 4) % 4, gz),
            (gx, gy, (gz + step + 8) % 8),
        )[f // 2])

    plane_order = [10, 9, 11, 6, 14, 2, 8, 5, 7, 13, 15, 1, 3, 4, 12]
    z_order = [4, 3, 5, 2, 6, 1, 7]

    barrier = pltpu.get_barrier_semaphore()
    peers = [sibling] + [plane_peer(d)[1] for d in plane_order] + [z_peer(d) for d in z_order] + ghost_to
    for peer in peers:
        pl.semaphore_signal(barrier, inc=1, device_id=peer, device_id_type=MESH)
    pl.semaphore_wait(barrier, len(peers))

    def remote(src, dst, send, recv, peer):
        return pltpu.make_async_remote_copy(
            src_ref=src, dst_ref=dst, send_sem=send, recv_sem=recv, device_id=peer, device_id_type=MESH
        )

    pair = remote(pack_ref.at[pl.ds((1 - c) * 16, 16)], pair_buf, pair_s, pair_r, sibling)
    pair.start()
    ghost_copies = []
    for f in range(FACES):
        cp = remote(ghost_ref.at[f], gbuf.at[f], g_s.at[f], g_r.at[f], ghost_to[f])
        cp.start()
        ghost_copies.append(cp)
    pair.wait_recv()
    half[...] = pack_ref[pl.ds(c * 16, 16)] + pair_buf[...]

    copies = []
    for d in plane_order:
        index, peer = plane_peer(d)
        cp = remote(half.at[index], plane_buf.at[d], plane_s.at[d], plane_r.at[d], peer)
        cp.start()
        copies.append(cp)

    total = local_ref[...]
    for f in range(FACES):
        ghost_copies[f].wait_recv()
        got = gbuf[f]
        high = got.astype(BF)
        low = (got - high.astype(F32)).astype(BF)
        ids = jnp.broadcast_to(rows_ref[f : f + 1], (NODES, SLOTS))
        hot = jnp.where(ids == lax.broadcasted_iota(jnp.int32, (NODES, SLOTS), 0), 1.0, 0.0).astype(BF)
        total = total + (mm(hot, high) + mm(hot, low))
    node_ref[...] = total

    own = half[plane]
    for cp in copies:
        cp.wait_recv()
    for d in range(1, 16):
        own = own + plane_buf[d]
    zbuf[z] = own
    z_copies = []
    for d in z_order:
        cp = remote(zbuf.at[z], zbuf.at[z], z_s.at[d], z_r.at[d], z_peer(d))
        cp.start()
        z_copies.append(cp)
    for cp in z_copies:
        cp.wait_recv()
    own = zbuf[0]
    for d in range(1, 8):
        own = own + zbuf[d]
    mine = c * 16 + plane
    fin[mine] = own

    gathers = []
    for d in plane_order:
        _, peer = plane_peer(d)
        cp = remote(fin.at[mine], fin.at[mine], ag_s.at[d], ag_r.at[d], peer)
        cp.start()
        gathers.append(cp)
    backs = []
    cp = remote(fin.at[mine], fin.at[mine], back_s.at[0], back_r.at[0], sibling)
    cp.start()
    backs.append(cp)
    for d, cp in reversed(list(zip(plane_order, gathers))):
        cp.wait_recv()
        source = c * 16 + plane_peer(16 - d if d % 4 == 0 else (4 - d // 4) % 4 * 4 + 4 - d % 4)[0]
        cp = remote(fin.at[source], fin.at[source], back_s.at[d], back_r.at[d], sibling)
        cp.start()
        backs.append(cp)
    for cp in backs:
        cp.wait_recv()
    out_ref[...] = fin[...]

    pair.wait_send()
    for cp in ghost_copies + copies + z_copies + gathers + backs:
        cp.wait_send()


def exchange(pack, ghost, local, rows):
    return pl.pallas_call(
        comm_kernel,
        out_shape=(
            jax.ShapeDtypeStruct((PIECES, PIECE, D), F32),
            jax.ShapeDtypeStruct((NODES, D), F32),
        ),
        in_specs=[VMEM] * 4,
        out_specs=(VMEM,) * 2,
        scratch_shapes=[
            pltpu.VMEM((16, PIECE, D), F32),
            pltpu.VMEM((16, PIECE, D), F32),
            pltpu.VMEM((16, PIECE, D), F32),
            pltpu.VMEM((8, PIECE, D), F32),
            pltpu.VMEM((PIECES, PIECE, D), F32),
            pltpu.VMEM((FACES, SLOTS, D), F32),
            pltpu.SemaphoreType.DMA,
            pltpu.SemaphoreType.DMA,
            pltpu.SemaphoreType.DMA((16,)),
            pltpu.SemaphoreType.DMA((16,)),
            pltpu.SemaphoreType.DMA((8,)),
            pltpu.SemaphoreType.DMA((8,)),
            pltpu.SemaphoreType.DMA((16,)),
            pltpu.SemaphoreType.DMA((16,)),
            pltpu.SemaphoreType.DMA((16,)),
            pltpu.SemaphoreType.DMA((16,)),
            pltpu.SemaphoreType.DMA((6,)),
            pltpu.SemaphoreType.DMA((6,)),
        ],
        compiler_params=pltpu.CompilerParams(collective_id=0, has_side_effects=True, vmem_limit_bytes=24 * 2**20),
        cost_estimate=pl.CostEstimate(flops=300_000_000, bytes_accessed=2_000_000, transcendentals=0),
    )(pack, ghost, local, rows)


def unpack_kernel(pack_ref, node_in, node_out, ew1, ewh, eb, eg, es, nw1, nwh, nb, ng):
    node_out[0, 0, 0] = node_in[...]
    ew1[...] = pack_ref[ROW_EW1 : ROW_EW1 + 3 * D]
    ewh[0] = pack_ref[ROW_EWH : ROW_EWH + D]
    ewh[1] = pack_ref[ROW_EWH + D : ROW_EWH + 2 * D]
    nw1[...] = pack_ref[ROW_NW1 : ROW_NW1 + 2 * D]
    nwh[0] = pack_ref[ROW_NWH : ROW_NWH + D]
    nwh[1] = pack_ref[ROW_NWH + D : ROW_NWH + 2 * D]
    eb[...] = pack_ref[ROW_ESM : ROW_ESM + 3]
    eg[...] = pack_ref[ROW_ESM + 3 : ROW_ESM + 4].reshape(D)
    es[...] = pack_ref[ROW_ESM + 4 : ROW_ESM + 5].reshape(D)
    nb[...] = pack_ref[ROW_NSM : ROW_NSM + 3]
    ng[...] = pack_ref[ROW_NSM + 3 : ROW_NSM + 4].reshape(D)


def unpack(pack, node):
    shapes = ((1, 1, 1, NODES, D), (3 * D, D), (2, D, D), (3, D), (D,), (D,), (2 * D, D), (2, D, D), (3, D), (D,))
    return pl.pallas_call(
        unpack_kernel,
        out_shape=tuple(jax.ShapeDtypeStruct(s, F32) for s in shapes),
        in_specs=[VMEM] * 2,
        out_specs=(VMEM,) * len(shapes),
        compiler_params=pltpu.CompilerParams(vmem_limit_bytes=8 * 2**20),
        cost_estimate=pl.CostEstimate(flops=1_000_000, bytes_accessed=2_000_000, transcendentals=0),
    )(pack, node)


def on_device(
    node_latent, ghost_latent, edge_latent, senders, receivers, export_rows, node_cotangent, edge_cotangent,
    w_edge_in, w_edge_hidden, b_edge, gain_edge, shift_edge, w_node_in, w_node_hidden, b_node, gain_node,
):
    devices = lax.axis_size("gx") * lax.axis_size("gy") * lax.axis_size("gz")
    scales = (float(EDGES * devices) ** (-0.5), float(NODES * devices) ** (-0.5))
    local, ghost, edge_grad, pack = local_compute(
        (
            node_latent, ghost_latent, edge_latent, senders, receivers, node_cotangent, edge_cotangent,
            w_edge_in, w_edge_hidden, b_edge, gain_edge, shift_edge, w_node_in, w_node_hidden, b_node, gain_node,
        ),
        scales,
    )
    summed, node = exchange(pack.reshape(PIECES, PIECE, D), ghost, local, export_rows.reshape(FACES, SLOTS))
    out = unpack(summed.reshape(ROWS, D), node)
    return (out[0], edge_grad) + tuple(out[1:])


def solution(mesh):
    block = lambda dims: P("gx", "gy", "gz", *([None] * dims))
    in_specs = tuple(block(k) for k in (2, 3, 2, 1, 1, 2, 2, 2)) + (P(),) * 9
    out_specs = (block(2), block(2)) + (P(),) * 9
    return jax.shard_map(on_device, mesh=mesh, in_specs=in_specs, out_specs=out_specs, check_vma=False)
```

time: 397 us -> 71.8 us (0.18)
  waiting for transfers between devices: 154 us -> 0 us
  other arithmetic: 82.4 us -> 0 us
  blocking collectives: 80.1 us -> 0 us
  Pallas kernels: 0 us -> 59.5 us
  local copies, waits for them, and re-layouts: 39.8 us -> 11.1 us
  matrix products: 14.9 us -> 0 us
  between operations: 14.8 us -> 0.69 us
  starting transfers between devices: 10.1 us -> 0 us
    psum x1 -> x0, waiting for transfers between devices: 154 us -> none  [on_device(): summed = tuple(lax.psum(edge_weights + node_weights, ('gx', 'gy', 'gz')))]
    psum x1 -> x0, blocking collectives: 80.1 us -> none  [on_device(): summed = tuple(lax.psum(edge_weights + node_weights, ('gx', 'gy', 'gz')))]
    scatter-add x9 -> x0, other arithmetic: 61.1 us -> none  [the longest x1 19.6 us: forward_states(): jax.ops.segment_sum(edge_new.astype(jnp.float32), receiver_ids, num_segme...]
    pallas_call x0 -> x3, Pallas kernels: none -> 59.5 us  [the longest x1 32.9 us: exchange(): pl.pallas_call(comm_kernel, out_shape=(jax.ShapeDtypeStruct((PIECES, PIEC...]
    gather x4 -> x0, local copies, waits for them, and re-layouts: 18.9 us -> none  [the longest x2 7.74 us: edge_backward_inputs(): new_grad = edge_upstream + agg_grad[receiver_ids]]
    dot_general x18 -> x0, matrix products: 14.9 us -> none  [the longest x12 10.7 us: matmul(): return jnp.dot(left, right, preferred_element_type=jnp.float32)]
    ppermute x6 -> x0, starting transfers between devices: 10 us -> none  [from_behind(): return lax.ppermute(x, axis, [(i, (i + by) % peers) for i in range(peers)])]
    mul x9 -> x0, other arithmetic: 9.03 us -> none  [the longest x1 1.62 us: on_device(): edge_weights[0] * edge_scale]
  transfers between devices with their start and end apart: 7 -> 0, of which waited for: 1 -> 0; matrix products, arithmetic and copies ran while one was open for 6% -> 0% of each run, Pallas kernels for 0% -> 0%
where the time goes in v1:
time: 71.8 us; the launch traced here: 71.3 us
  Pallas kernels  59.5 us (83%)
  local copies, waits for them, and re-layouts  11.1 us (15%)
    pallas_call x1, Pallas kernels, exchange(): pl.pallas_call(comm_kernel, out_shape=(jax.ShapeDtypeStruct((PIECES, PIEC...  32.9 us
    pallas_call x1, Pallas kernels, local_compute(): pl.pallas_call(functools.partial(compute_kernel, scales), out_shape=(jax....  25.6 us
    unnamed x33, local copies, waits for them, and re-layouts  11.1 us

profile of v1, /device:TPU:1, one launch (start us, length us, event | category | flops | bytes accessed | tf_op | source)
XLA Modules:
  0.0 71.3 jit_solution(13088467867392152137)
XLA Ops:
  0.6 0.0 copy-start.12
  0.7 0.0 copy-start.11
  0.7 0.7 copy.30
  1.4 0.0 copy-start.13
  1.4 0.0 copy-start.14
  1.4 0.0 copy-start.15
  1.4 0.0 copy-done.12
  1.4 0.0 copy-done.11
  1.4 0.6 copy-done.13
  2.0 0.0 copy-done.14
  2.0 0.0 copy-done.15
  2.0 0.0 copy-start
  2.1 1.1 %copy-done = bf16[1,1,1,2816,128]{4,3,2,1,0:T(8,128)(2,1)S(1)} copy-done((bf16[1,1,1,2816,128]{4,3,2,1,0:T(8,128)(2,1)S(1)}, bf16[1,1,1,2816,128]{4,3,2,1,0:T(8,128)(2,1)}, u32[]{:S(2)}) %copy-start) | copy-done | bytes 720920
  3.2 0.0 copy-start.1
  3.2 1.1 %copy-done.1 = bf16[1,1,1,2816,128]{4,3,2,1,0:T(8,128)(2,1)S(1)} copy-done((bf16[1,1,1,2816,128]{4,3,2,1,0:T(8,128)(2,1)S(1)}, bf16[1,1,1,2816,128]{4,3,2,1,0:T(8,128)(2,1)}, u32[]{:S(2)}) %copy-start.1) | copy-done | bytes 720920
  4.3 0.0 copy-start.2
  4.3 0.9 %copy-done.2 = bf16[1,1,1,512,128]{4,3,2,1,0:T(8,128)(2,1)S(1)} copy-done((bf16[1,1,1,512,128]{4,3,2,1,0:T(8,128)(2,1)S(1)}, bf16[1,1,1,512,128]{4,3,2,1,0:T(8,128)(2,1)}, u32[]{:S(2)}) %copy-start.2) | copy-done | bytes 131096
  5.2 0.0 copy-start.3
  5.2 0.9 %copy-done.3 = bf16[1,1,1,512,128]{4,3,2,1,0:T(8,128)(2,1)S(1)} copy-done((bf16[1,1,1,512,128]{4,3,2,1,0:T(8,128)(2,1)S(1)}, bf16[1,1,1,512,128]{4,3,2,1,0:T(8,128)(2,1)}, u32[]{:S(2)}) %copy-start.3) | copy-done | bytes 131096
  6.1 0.0 copy-start.4
  6.1 0.9 %copy-done.4 = bf16[1,1,1,6,64,128]{5,4,3,2,1,0:T(8,128)(2,1)S(1)} copy-done((bf16[1,1,1,6,64,128]{5,4,3,2,1,0:T(8,128)(2,1)S(1)}, bf16[1,1,1,6,64,128]{5,4,3,2,1,0:T(8,128)(2,1)}, u32[]{:S(2)}) %copy-start.4) | copy-done | bytes 98328
  7.0 0.0 copy-start.5
  7.0 0.9 %copy-done.5 = bf16[384,128]{1,0:T(8,128)(2,1)S(1)} copy-done((bf16[384,128]{1,0:T(8,128)(2,1)S(1)}, bf16[384,128]{1,0:T(8,128)(2,1)}, u32[]{:S(2)}) %copy-start.5) | copy-done | bytes 98328
  7.9 0.0 copy-start.6
  7.9 0.8 %copy-done.6 = bf16[2,128,128]{2,1,0:T(8,128)(2,1)S(1)} copy-done((bf16[2,128,128]{2,1,0:T(8,128)(2,1)S(1)}, bf16[2,128,128]{2,1,0:T(8,128)(2,1)}, u32[]{:S(2)}) %copy-start.6) | copy-done | bytes 65560
  8.7 0.0 copy-start.7
  8.7 0.8 %copy-done.7 = bf16[256,128]{1,0:T(8,128)(2,1)S(1)} copy-done((bf16[256,128]{1,0:T(8,128)(2,1)S(1)}, bf16[256,128]{1,0:T(8,128)(2,1)}, u32[]{:S(2)}) %copy-start.7) | copy-done | bytes 65560
  9.5 0.0 copy-start.8
  9.5 0.8 %copy-done.8 = bf16[2,128,128]{2,1,0:T(8,128)(2,1)S(1)} copy-done((bf16[2,128,128]{2,1,0:T(8,128)(2,1)S(1)}, bf16[2,128,128]{2,1,0:T(8,128)(2,1)}, u32[]{:S(2)}) %copy-start.8) | copy-done | bytes 65560
  10.4 0.0 copy-start.9
  10.4 0.7 copy-done.9
  11.1 0.0 copy-start.10
  11.1 0.7 copy-done.10
  11.8 25.6 %shard_map.248 = (f32[512,128]{1,0:T(8,128)S(1)}, f32[6,64,128]{2,1,0:T(8,128)S(1)}, bf16[1,1,1,2816,128]{4,3,2,1,0:T(8,128)(2,1)}, f32[1280,128]{1,0:T(8,128)S(1)}) custom-call(bf16[1,1,1,512,128]{4,3,2,1,0:T(8,128)(2,1)S(1)} %copy-done.2, bf16[1,1,1,6,64,128]{5,4,3,2,1,0:T(8,128)(2,1)S(1)} %copy-done.4, bf16[1,1,1,2816,128]{4,3,2,1,0:T(8,128)(2,1)S(1)} %copy-done, ...), custom_call_target="tpu_custom_call" | custom-call | flops 6000000000 | bytes 6000000 | tf_op jit(solution)/shard_map/pallas_call | solution.py:226
  37.4 32.9 %shard_map.249 = (f32[32,40,128]{2,1,0:T(8,128)S(1)}, f32[512,128]{1,0:T(8,128)S(1)}) custom-call(f32[32,40,128]{2,1,0:T(8,128)S(1)} %bitcast.6, f32[6,64,128]{2,1,0:T(8,128)S(1)} %get-tuple-element.28.ghost_ref, f32[512,128]{1,0:T(8,128)S(1)} %get-tuple-element.29.local_ref, s32[6,64]{1,0:T(8,128)S(1)} %bitcast.7), custom_call_target="tpu_custom_call" | custom-call | flops 300000000 | bytes 2000000 | tf_op jit(solution)/shard_map/pallas_call | solution.py:376
  70.3 1.0 %shard_map.250 = (f32[1,1,1,512,128]{4,3,2,1,0:T(8,128)}, f32[384,128]{1,0:T(8,128)}, f32[2,128,128]{2,1,0:T(8,128)}, f32[3,128]{1,0:T(4,128)}, f32[128]{0:T(128...) custom-call(f32[1280,128]{1,0:T(8,128)S(1)} %bitcast.5, ...), custom_call_target="tpu_custom_call" | custom-call | flops 1000000 | bytes 2000000 | tf_op jit(solution)/shard_map/pallas_call | solution.py:426
Async XLA Ops:
  0.6 0.7 %copy-start.12 = (f32[3,128]{1,0:T(4,128)S(1)}, f32[3,128]{1,0:T(4,128)}, u32[]{:S(2)}) copy-start(f32[3,128]{1,0:T(4,128)} %nb_ref.1) | copy-start | bytes 4612
  0.7 0.7 %copy-start.11 = (f32[3,128]{1,0:T(4,128)S(1)}, f32[3,128]{1,0:T(4,128)}, u32[]{:S(2)}) copy-start(f32[3,128]{1,0:T(4,128)} %eb_ref.1) | copy-start | bytes 4612
  1.4 0.7 copy-start.13
  1.4 0.7 copy-start.14
  1.4 0.7 copy-start.15
  2.0 1.1 %copy-start = (bf16[1,1,1,2816,128]{4,3,2,1,0:T(8,128)(2,1)S(1)}, bf16[1,1,1,2816,128]{4,3,2,1,0:T(8,128)(2,1)}, u32[]{:S(2)}) copy-start(bf16[1,1,1,2816,128]{4,3,2,1,0:T(8,128)(2,1)} %edge_ref.1) | copy-start | bytes 2162692
  3.2 1.1 %copy-start.1 = (bf16[1,1,1,2816,128]{4,3,2,1,0:T(8,128)(2,1)S(1)}, bf16[1,1,1,2816,128]{4,3,2,1,0:T(8,128)(2,1)}, u32[]{:S(2)}) copy-start(bf16[1,1,1,2816,128]{4,3,2,1,0:T(8,128)(2,1)} %ecot_ref.1) | copy-start | bytes 2162692
  4.3 0.9 %copy-start.2 = (bf16[1,1,1,512,128]{4,3,2,1,0:T(8,128)(2,1)S(1)}, bf16[1,1,1,512,128]{4,3,2,1,0:T(8,128)(2,1)}, u32[]{:S(2)}) copy-start(bf16[1,1,1,512,128]{4,3,2,1,0:T(8,128)(2,1)} %node_ref.1) | copy-start | bytes 393220
  5.2 0.9 %copy-start.3 = (bf16[1,1,1,512,128]{4,3,2,1,0:T(8,128)(2,1)S(1)}, bf16[1,1,1,512,128]{4,3,2,1,0:T(8,128)(2,1)}, u32[]{:S(2)}) copy-start(bf16[1,1,1,512,128]{4,3,2,1,0:T(8,128)(2,1)} %ncot_ref.1) | copy-start | bytes 393220
  6.1 0.9 %copy-start.4 = (bf16[1,1,1,6,64,128]{5,4,3,2,1,0:T(8,128)(2,1)S(1)}, bf16[1,1,1,6,64,128]{5,4,3,2,1,0:T(8,128)(2,1)}, u32[]{:S(2)}) copy-start(bf16[1,1,1,6,64,128]{5,4,3,2,1,0:T(8,128)(2,1)} %ghost_ref.1) | copy-start | bytes 294916
  7.0 0.9 %copy-start.5 = (bf16[384,128]{1,0:T(8,128)(2,1)S(1)}, bf16[384,128]{1,0:T(8,128)(2,1)}, u32[]{:S(2)}) copy-start(bf16[384,128]{1,0:T(8,128)(2,1)} %ew1_ref.1) | copy-start | bytes 294916
  7.9 0.8 %copy-start.6 = (bf16[2,128,128]{2,1,0:T(8,128)(2,1)S(1)}, bf16[2,128,128]{2,1,0:T(8,128)(2,1)}, u32[]{:S(2)}) copy-start(bf16[2,128,128]{2,1,0:T(8,128)(2,1)} %ewh_ref.1) | copy-start | bytes 196612
  8.7 0.8 %copy-start.7 = (bf16[256,128]{1,0:T(8,128)(2,1)S(1)}, bf16[256,128]{1,0:T(8,128)(2,1)}, u32[]{:S(2)}) copy-start(bf16[256,128]{1,0:T(8,128)(2,1)} %nw1_ref.1) | copy-start | bytes 196612
  9.5 0.8 %copy-start.8 = (bf16[2,128,128]{2,1,0:T(8,128)(2,1)S(1)}, bf16[2,128,128]{2,1,0:T(8,128)(2,1)}, u32[]{:S(2)}) copy-start(bf16[2,128,128]{2,1,0:T(8,128)(2,1)} %nwh_ref.1) | copy-start | bytes 196612
  10.4 0.7 copy-start.9
  11.1 0.7 copy-start.10

commit v2 on v1

v2 whole, which is shorter than its diff:
```python
import functools

import jax
import jax.numpy as jnp
from jax import lax
from jax.experimental import pallas as pl
from jax.experimental.pallas import tpu as pltpu
from jax.sharding import PartitionSpec as P

EPSILON = 1e-05
MESH = pl.DeviceIdType.MESH
BF = jnp.bfloat16
F32 = jnp.float32
D = 128
NODES = 512
FACES = 6
SLOTS = 64
FULL = NODES + FACES * SLOTS
EDGES = 2816
CH = 1408
CHUNKS = EDGES // CH
SEND_TILES = FULL // D
RECV_TILES = NODES // D
TILES = SEND_TILES + RECV_TILES
PIECES = 32
PIECE = 40
ROW_EW1 = 0
ROW_EWH = 384
ROW_ESM = 640
ROW_NW1 = 648
ROW_NWH = 904
ROW_NSM = 1160
ROWS = PIECES * PIECE
PLANE_ORDER = (10, 9, 11, 6, 14, 2, 8, 5, 7, 13, 15, 1, 3, 4, 12)
Z_ORDER = (4, 3, 5, 2, 6, 1, 7)


def mm(a, b):
    return jnp.dot(a, b, preferred_element_type=F32)


def mm_tn(a, b):
    return lax.dot_general(a, b, (((0,), (0,)), ((), ())), preferred_element_type=F32)


def transposed(w):
    return w.astype(F32).T.astype(BF)


def silu_parts(p):
    s = 0.5 * jnp.tanh(0.5 * p) + 0.5
    z = p * s
    return z, s + z * (1.0 - s)


def norm_parts(p):
    c = p - jnp.mean(p, -1, keepdims=True)
    inv = lax.rsqrt(jnp.mean(c * c, -1, keepdims=True) + EPSILON)
    return c * inv, inv


def norm_back(u, gain, n, inv):
    t = u * gain
    return inv * (t - jnp.mean(t, -1, keepdims=True) - n * jnp.mean(t * n, -1, keepdims=True))


def fold(x):
    return jnp.sum(x.reshape(x.shape[0] // 8, 8, x.shape[1]), 0)


def row_sum(x):
    return jnp.sum(fold(x), 0, keepdims=True)


def column_digits(ids_row):
    lo, hi = [], []
    for j in range(ids_row.shape[1] // D):
        t = jnp.broadcast_to(ids_row[:, j * D : (j + 1) * D], (D, D)).T
        lo.append((t & (D - 1)).astype(F32).astype(BF))
        hi.append((t >> 7).astype(F32).astype(BF))
    return jnp.concatenate(lo, 0), jnp.concatenate(hi, 0)


def one_hot_columns(lo, hi, tiles):
    lane = lax.broadcasted_iota(jnp.int32, lo.shape, 1).astype(F32).astype(BF)
    zero = jnp.zeros(lo.shape, BF)
    base = jnp.where(lo == lane, jnp.ones(lo.shape, BF), zero)
    return [jnp.where(hi == BF(k), base, zero) for k in range(tiles)]


def one_hot_rows(ids_row, tiles):
    n = ids_row.shape[1]
    lo = jnp.broadcast_to((ids_row & (D - 1)).astype(F32), (D, n)).astype(BF)
    hi = jnp.broadcast_to((ids_row >> 7).astype(F32), (D, n)).astype(BF)
    row = lax.broadcasted_iota(jnp.int32, (D, n), 0).astype(F32).astype(BF)
    zero = jnp.zeros((D, n), BF)
    base = jnp.where(lo == row, jnp.ones((D, n), BF), zero)
    return [jnp.where(hi == BF(k), base, zero) for k in range(tiles)]


class Exchange:
    def __init__(self, refs):
        (
            self.pack, self.pair_buf, self.half, self.plane_buf, self.zbuf, self.fin, self.gbuf,
            self.pair_s, self.pair_r, self.plane_s, self.plane_r, self.z_s, self.z_r,
            self.ag_s, self.ag_r, self.back_s, self.back_r, self.g_s, self.g_r,
        ) = refs
        gx, gy, gz = lax.axis_index("gx"), lax.axis_index("gy"), lax.axis_index("gz")
        self.y, self.zl = gx // 2, gx % 2
        self.x, self.c = gz // 2, gz % 2
        self.z = gy * 2 + self.zl
        self.at = (gx, gy, gz)
        self.plane = self.x * 4 + self.y
        self.sibling = (gx, gy, gz + 1 - 2 * self.c)
        self.started = []
        self.ghost_to = []
        for f in range(FACES):
            step = 1 if f % 2 == 0 else -1
            self.ghost_to.append((
                ((gx + step + 8) % 8, gy, gz),
                (gx, (gy + step + 4) % 4, gz),
                (gx, gy, (gz + step + 8) % 8),
            )[f // 2])

    def plane_peer(self, d):
        px, py = (self.x + d // 4) % 4, (self.y + d % 4) % 4
        return px * 4 + py, (py * 2 + self.zl, self.at[1], px * 2 + self.c)

    def z_peer(self, d):
        pz = (self.z + d) % 8
        return (self.y * 2 + pz % 2, pz // 2, self.at[2])

    def greet(self):
        barrier = pltpu.get_barrier_semaphore()
        peers = [self.sibling] + [self.plane_peer(d)[1] for d in PLANE_ORDER]
        peers += [self.z_peer(d) for d in Z_ORDER] + self.ghost_to
        for peer in peers:
            pl.semaphore_signal(barrier, inc=1, device_id=peer, device_id_type=MESH)
        self.greeted = len(peers)

    def remote(self, src, dst, send, recv, peer):
        cp = pltpu.make_async_remote_copy(
            src_ref=src, dst_ref=dst, send_sem=send, recv_sem=recv, device_id=peer, device_id_type=MESH
        )
        cp.start()
        self.started.append(cp)
        return cp

    def swap_halves(self):
        pl.semaphore_wait(pltpu.get_barrier_semaphore(), self.greeted)
        self.pair = self.remote(
            self.pack.at[pl.ds((1 - self.c) * 16, 16)], self.pair_buf, self.pair_s, self.pair_r, self.sibling
        )

    def reduce_in_plane(self):
        self.pair.wait_recv()
        self.half[...] = self.pack[pl.ds(self.c * 16, 16)] + self.pair_buf[...]
        self.in_plane = []
        for d in PLANE_ORDER:
            index, peer = self.plane_peer(d)
            self.in_plane.append(
                self.remote(self.half.at[index], self.plane_buf.at[d], self.plane_s.at[d], self.plane_r.at[d], peer)
            )

    def send_ghosts(self, ghost_ref):
        self.ghosts = [
            self.remote(ghost_ref.at[f], self.gbuf.at[f], self.g_s.at[f], self.g_r.at[f], self.ghost_to[f])
            for f in range(FACES)
        ]

    def reduce_along_z(self):
        own = self.half[self.plane]
        for cp in self.in_plane:
            cp.wait_recv()
        for d in range(1, 16):
            own = own + self.plane_buf[d]
        self.zbuf[self.z] = own
        self.along_z = [
            self.remote(self.zbuf.at[self.z], self.zbuf.at[self.z], self.z_s.at[d], self.z_r.at[d], self.z_peer(d))
            for d in Z_ORDER
        ]

    def add_ghosts(self, total, rows_ref):
        for f in range(FACES):
            self.ghosts[f].wait_recv()
            got = self.gbuf[f]
            high = got.astype(BF)
            low = (got - high.astype(F32)).astype(BF)
            ids = jnp.broadcast_to(rows_ref[f], (NODES, SLOTS))
            hot = jnp.where(ids == lax.broadcasted_iota(jnp.int32, (NODES, SLOTS), 0), 1.0, 0.0).astype(BF)
            total = total + (mm(hot, high) + mm(hot, low))
        return total

    def spread(self):
        for cp in self.along_z:
            cp.wait_recv()
        own = self.zbuf[0]
        for d in range(1, 8):
            own = own + self.zbuf[d]
        mine = self.c * 16 + self.plane
        self.fin[mine] = own
        piece = self.fin.at[mine]
        gathers = [
            self.remote(piece, piece, self.ag_s.at[d], self.ag_r.at[d], self.plane_peer(d)[1]) for d in PLANE_ORDER
        ]
        backs = [self.remote(piece, piece, self.back_s.at[0], self.back_r.at[0], self.sibling)]
        for d, cp in reversed(list(zip(PLANE_ORDER, gathers))):
            cp.wait_recv()
            source = (4 - d // 4) % 4 * 4 + (4 - d % 4) % 4
            piece = self.fin.at[self.c * 16 + self.plane_peer(source)[0]]
            backs.append(self.remote(piece, piece, self.back_s.at[d], self.back_r.at[d], self.sibling))
        for cp in backs:
            cp.wait_recv()

    def drain(self):
        for cp in self.started:
            cp.wait_send()


def fused_kernel(scales, *refs):
    inputs, refs = refs[:INPUTS], refs[INPUTS:]
    edge_out_ref, out_ref, node_out_ref = refs[:3]
    held, refs = refs[3 : 3 + INPUTS], refs[3 + INPUTS :]
    in_sem = refs[0]
    (
        table, z1, z2, sl1, sl2, nrm, inv, rlo, rhi, agg, acc, w3t, w2t, w1t, aggb, small,
        local_ref, ghost_out_ref, pack_ref,
    ) = refs[1:20]
    comm_refs = refs[20:]
    loads = [pltpu.make_async_copy(a, b, in_sem.at[k]) for k, (a, b) in enumerate(zip(inputs, held))]
    for cp in loads:
        cp.start()
    comm = Exchange(comm_refs)
    comm.greet()
    (
        node_ref, ghost_ref, ew1_ref, ewh_ref, send_ref, recv_ref, edge_ref, eb_ref, eg_ref, es_ref,
        nw1_ref, nwh_ref, nb_ref, ng_ref, ncot_ref, ecot_ref, rows_ref,
    ) = held
    edge_scale, node_scale = scales
    for cp in loads[:4]:
        cp.wait()
    node = node_ref[0, 0, 0]
    ghosts = ghost_ref[0, 0, 0].reshape(FACES * SLOTS, D)
    full = jnp.concatenate([node, ghosts], 0)
    table[0:FULL] = mm(full, ew1_ref[D : 2 * D]).astype(BF)
    table[FULL : FULL + NODES] = mm(node, ew1_ref[2 * D : 3 * D]).astype(BF)
    table[FULL + NODES :] = ew1_ref[0:D]
    w3t[...] = transposed(ewh_ref[1])
    w2t[...] = transposed(ewh_ref[0])
    w1t[...] = transposed(ew1_ref[0:D])
    agg[...] = jnp.zeros_like(agg)
    acc[...] = jnp.zeros_like(acc)
    small[...] = jnp.zeros_like(small)
    pack_ref[...] = jnp.zeros_like(pack_ref)
    for cp in loads[4:10]:
        cp.wait()
    egain = eg_ref[...].reshape(1, D)
    eshift = es_ref[...].reshape(1, D)

    def forward(i, carry):
        off = pl.multiple_of(i * CH, CH)
        rows = pl.ds(off, CH)
        s_row = send_ref[0, 0, :, rows]
        r_row = recv_ref[0, 0, :, rows]
        slo, shi = column_digits(s_row)
        lo, hi = column_digits(r_row)
        rlo[rows] = lo
        rhi[rows] = hi
        hot = one_hot_columns(slo, shi, SEND_TILES) + one_hot_columns(lo, hi, RECV_TILES)
        lhs = jnp.concatenate(hot + [edge_ref[0, 0, 0, rows]], 1)
        p1 = mm(lhs, table[...]) + eb_ref[0:1]
        a1, d1 = silu_parts(p1)
        b1 = a1.astype(BF)
        z1[rows] = b1
        sl1[rows] = d1
        p2 = mm(b1, ewh_ref[0]) + eb_ref[1:2]
        a2, d2 = silu_parts(p2)
        b2 = a2.astype(BF)
        z2[rows] = b2
        sl2[rows] = d2
        q = mm(b2, ewh_ref[1]) + eb_ref[2:3]
        n, iv = norm_parts(q)
        nrm[rows] = n
        inv[rows] = jnp.broadcast_to(iv, (CH, D))
        new = (n * egain + eshift).astype(BF)
        hot_t = jnp.concatenate(one_hot_rows(r_row, RECV_TILES), 0)
        agg[...] += mm(hot_t, new)
        return carry

    lax.fori_loop(0, CHUNKS, forward, 0)

    for cp in loads[10:]:
        cp.wait()
    ngain = ng_ref[...].reshape(1, D)
    node_in = jnp.concatenate([node, agg[...].astype(BF)], 1)
    a1, d1 = silu_parts(mm(node_in, nw1_ref[...]) + nb_ref[0:1])
    b1 = a1.astype(BF)
    a2, d2 = silu_parts(mm(b1, nwh_ref[0]) + nb_ref[1:2])
    b2 = a2.astype(BF)
    n, iv = norm_parts(mm(b2, nwh_ref[1]) + nb_ref[2:3])
    u = ncot_ref[0, 0, 0].astype(F32)
    g3 = norm_back(u, ngain, n, iv)
    h3 = g3.astype(BF)
    g2 = mm(h3, transposed(nwh_ref[1])) * d2
    h2 = g2.astype(BF)
    g1 = mm(h2, transposed(nwh_ref[0])) * d1
    h1 = g1.astype(BF)
    local_ref[...] = u + mm(h1, transposed(nw1_ref[0:D]))
    aggb[...] = mm(h1, transposed(nw1_ref[D : 2 * D])).astype(BF)
    pack_ref[ROW_NW1 : ROW_NW1 + 2 * D] = mm_tn(node_in, h1) * node_scale
    pack_ref[ROW_NWH : ROW_NWH + D] = mm_tn(b1, h2) * node_scale
    pack_ref[ROW_NWH + D : ROW_NWH + 2 * D] = mm_tn(b2, h3) * node_scale
    pack_ref[ROW_NSM : ROW_NSM + 4] = node_scale * jnp.concatenate(
        [row_sum(g1), row_sum(g2), row_sum(g3), row_sum(u * n)], 0
    )

    def backward(i, carry):
        off = pl.multiple_of(i * CH, CH)
        rows = pl.ds(off, CH)
        s_row = send_ref[0, 0, :, rows]
        r_row = recv_ref[0, 0, :, rows]
        hot = jnp.concatenate(one_hot_columns(rlo[rows], rhi[rows], RECV_TILES), 1)
        cot = ecot_ref[0, 0, 0, rows].astype(F32)
        u = cot + mm(hot, aggb[...])
        n = nrm[rows]
        g3 = norm_back(u, egain, n, inv[rows])
        h3 = g3.astype(BF)
        g2 = mm(h3, w3t[...]) * sl2[rows]
        h2 = g2.astype(BF)
        g1 = mm(h2, w2t[...]) * sl1[rows]
        h1 = g1.astype(BF)
        edge_out_ref[0, 0, 0, rows] = (cot + mm(h1, w1t[...])).astype(BF)
        pack_ref[ROW_EW1 : ROW_EW1 + D] += mm_tn(edge_ref[0, 0, 0, rows], h1)
        pack_ref[ROW_EWH : ROW_EWH + D] += mm_tn(z1[rows], h2)
        pack_ref[ROW_EWH + D : ROW_EWH + 2 * D] += mm_tn(z2[rows], h3)
        hot_t = jnp.concatenate(one_hot_rows(s_row, SEND_TILES) + one_hot_rows(r_row, RECV_TILES), 0)
        acc[...] += mm(hot_t, h1)
        small[0] += fold(g1)
        small[1] += fold(g2)
        small[2] += fold(g3)
        small[3] += fold(u * n)
        small[4] += fold(u)
        return carry

    lax.fori_loop(0, CHUNKS, backward, 0)

    sums = acc[0:FULL].astype(BF)
    sums_r = acc[FULL : FULL + NODES].astype(BF)
    pack_ref[ROW_EW1 : ROW_EW1 + D] = pack_ref[ROW_EW1 : ROW_EW1 + D] * edge_scale
    pack_ref[ROW_EW1 + D : ROW_EW1 + 2 * D] = mm_tn(full, sums) * edge_scale
    pack_ref[ROW_EW1 + 2 * D : ROW_EW1 + 3 * D] = mm_tn(node, sums_r) * edge_scale
    pack_ref[ROW_EWH : ROW_EWH + 2 * D] = pack_ref[ROW_EWH : ROW_EWH + 2 * D] * edge_scale
    pack_ref[ROW_ESM : ROW_ESM + 5] = edge_scale * jnp.concatenate(
        [jnp.sum(small[j], 0, keepdims=True) for j in range(5)], 0
    )
    for p in range(PIECES):
        comm.pack[p] = pack_ref[p * PIECE : (p + 1) * PIECE]
    comm.swap_halves()
    back = mm(sums, transposed(ew1_ref[D : 2 * D]))
    local_ref[...] += back[0:NODES] + mm(sums_r, transposed(ew1_ref[2 * D : 3 * D]))
    ghost_out_ref[...] = back[NODES:].reshape(FACES, SLOTS, D)
    comm.reduce_in_plane()
    comm.send_ghosts(ghost_out_ref)
    comm.reduce_along_z()
    node_out_ref[...] = comm.add_ghosts(local_ref[...], rows_ref)
    comm.spread()
    out_ref[...] = comm.fin[...]
    comm.drain()


VMEM = pl.BlockSpec(memory_space=pltpu.VMEM)
HBM = pl.BlockSpec(memory_space=pltpu.HBM)
INPUTS = 17


def fused(args, scales):
    scratch = [pltpu.VMEM(a.shape, a.dtype) for a in args]
    scratch += [
        pltpu.SemaphoreType.DMA((INPUTS,)),
        pltpu.VMEM((FULL + NODES + D, D), BF),
        pltpu.VMEM((EDGES, D), BF),
        pltpu.VMEM((EDGES, D), BF),
        pltpu.VMEM((EDGES, D), F32),
        pltpu.VMEM((EDGES, D), F32),
        pltpu.VMEM((EDGES, D), F32),
        pltpu.VMEM((EDGES, D), F32),
        pltpu.VMEM((EDGES, D), BF),
        pltpu.VMEM((EDGES, D), BF),
        pltpu.VMEM((NODES, D), F32),
        pltpu.VMEM((FULL + NODES, D), F32),
        pltpu.VMEM((D, D), BF),
        pltpu.VMEM((D, D), BF),
        pltpu.VMEM((D, D), BF),
        pltpu.VMEM((NODES, D), BF),
        pltpu.VMEM((5, 8, D), F32),
        pltpu.VMEM((NODES, D), F32),
        pltpu.VMEM((FACES, SLOTS, D), F32),
        pltpu.VMEM((ROWS, D), F32),
        pltpu.VMEM((PIECES, PIECE, D), F32),
        pltpu.VMEM((16, PIECE, D), F32),
        pltpu.VMEM((16, PIECE, D), F32),
        pltpu.VMEM((16, PIECE, D), F32),
        pltpu.VMEM((8, PIECE, D), F32),
        pltpu.VMEM((PIECES, PIECE, D), F32),
        pltpu.VMEM((FACES, SLOTS, D), F32),
        pltpu.SemaphoreType.DMA,
        pltpu.SemaphoreType.DMA,
    ]
    for n in (16, 16, 8, 8, 16, 16, 16, 16, FACES, FACES):
        scratch.append(pltpu.SemaphoreType.DMA((n,)))
    return pl.pallas_call(
        functools.partial(fused_kernel, scales),
        out_shape=(
            jax.ShapeDtypeStruct((1, 1, 1, EDGES, D), BF),
            jax.ShapeDtypeStruct((PIECES, PIECE, D), F32),
            jax.ShapeDtypeStruct((NODES, D), F32),
        ),
        in_specs=[HBM] * INPUTS,
        out_specs=(VMEM,) * 3,
        scratch_shapes=scratch,
        compiler_params=pltpu.CompilerParams(collective_id=0, has_side_effects=True, vmem_limit_bytes=52 * 2**20),
        cost_estimate=pl.CostEstimate(flops=6_000_000_000, bytes_accessed=6_000_000, transcendentals=800_000),
    )(*[pltpu.with_memory_space_constraint(a, pltpu.HBM) for a in args])


def unpack_kernel(edge_in, pack_in, node_in, edge_out, node_out, ew1, ewh, nw1, nwh, eb, eg, es, nb, ng, sem):
    moves = (
        (edge_in, edge_out),
        (node_in, node_out.at[0, 0, 0]),
        (pack_in.at[ROW_EW1 : ROW_EW1 + 3 * D], ew1),
        (pack_in.at[ROW_EWH : ROW_EWH + D], ewh.at[0]),
        (pack_in.at[ROW_EWH + D : ROW_EWH + 2 * D], ewh.at[1]),
        (pack_in.at[ROW_NW1 : ROW_NW1 + 2 * D], nw1),
        (pack_in.at[ROW_NWH : ROW_NWH + D], nwh.at[0]),
        (pack_in.at[ROW_NWH + D : ROW_NWH + 2 * D], nwh.at[1]),
    )
    copies = [pltpu.make_async_copy(a, b, sem.at[k]) for k, (a, b) in enumerate(moves)]
    for cp in copies:
        cp.start()
    eb[...] = pack_in[ROW_ESM : ROW_ESM + 3]
    eg[...] = pack_in[ROW_ESM + 3 : ROW_ESM + 4].reshape(D)
    es[...] = pack_in[ROW_ESM + 4 : ROW_ESM + 5].reshape(D)
    nb[...] = pack_in[ROW_NSM : ROW_NSM + 3]
    ng[...] = pack_in[ROW_NSM + 3 : ROW_NSM + 4].reshape(D)
    for cp in copies:
        cp.wait()


def unpack(edge, pack, node):
    shapes = ((1, 1, 1, NODES, D), (3 * D, D), (2, D, D), (2 * D, D), (2, D, D), (3, D), (D,), (D,), (3, D), (D,))
    return pl.pallas_call(
        unpack_kernel,
        out_shape=(jax.ShapeDtypeStruct(edge.shape, BF),) + tuple(jax.ShapeDtypeStruct(s, F32) for s in shapes),
        in_specs=[VMEM] * 3,
        out_specs=(HBM,) * 6 + (VMEM,) * 5,
        scratch_shapes=[pltpu.SemaphoreType.DMA((8,))],
        compiler_params=pltpu.CompilerParams(vmem_limit_bytes=8 * 2**20),
        cost_estimate=pl.CostEstimate(flops=1_000_000, bytes_accessed=4_000_000, transcendentals=0),
    )(edge, pack, node)


def on_device(
    node_latent, ghost_latent, edge_latent, senders, receivers, export_rows, node_cotangent, edge_cotangent,
    w_edge_in, w_edge_hidden, b_edge, gain_edge, shift_edge, w_node_in, w_node_hidden, b_node, gain_node,
):
    devices = lax.axis_size("gx") * lax.axis_size("gy") * lax.axis_size("gz")
    scales = (float(EDGES * devices) ** (-0.5), float(NODES * devices) ** (-0.5))
    edge, summed, node = fused(
        (
            node_latent, ghost_latent, w_edge_in, w_edge_hidden, senders, receivers, edge_latent,
            b_edge, gain_edge, shift_edge, w_node_in, w_node_hidden, b_node, gain_node,
            node_cotangent, edge_cotangent, export_rows.reshape(FACES, 1, SLOTS),
        ),
        scales,
    )
    edge_grad, node_grad, ew1, ewh, nw1, nwh, eb, eg, es, nb, ng = unpack(edge, summed.reshape(ROWS, D), node)
    return (node_grad, edge_grad, ew1, ewh, eb, eg, es, nw1, nwh, nb, ng)


def solution(mesh):
    block = lambda dims: P("gx", "gy", "gz", *([None] * dims))
    in_specs = tuple(block(k) for k in (2, 3, 2, 1, 1, 2, 2, 2)) + (P(),) * 9
    out_specs = (block(2), block(2)) + (P(),) * 9
    return jax.shard_map(on_device, mesh=mesh, in_specs=in_specs, out_specs=out_specs, check_vma=False)
```

time: 71.8 us -> 48.9 us (0.68)
  Pallas kernels: 59.5 us -> 48.2 us
  local copies, waits for them, and re-layouts: 11.1 us -> 0 us
    pallas_call x3 -> x2, Pallas kernels: 59.5 us -> 48.2 us  [the longest x1 46.4 us: fused(): pl.pallas_call(functools.partial(fused_kernel, scales), out_shape=(jax.Sh...]
    unnamed x33 -> x0, local copies, waits for them, and re-layouts: 11.1 us -> none
where the time goes in v2:
time: 48.9 us; the launch traced here: 48.8 us
  Pallas kernels  48.2 us (99%)
  between operations  0.66 us (1%)
    pallas_call x1, Pallas kernels, fused(): pl.pallas_call(functools.partial(fused_kernel, scales), out_shape=(jax.Sh...  46.4 us
    pallas_call x1, Pallas kernels, unpack(): pl.pallas_call(unpack_kernel, out_shape=(jax.ShapeDtypeStruct(edge.shape,...  1.79 us

profile of v2, /device:TPU:1, one launch (start us, length us, event | category | flops | bytes accessed | tf_op | source)
XLA Modules:
  0.0 48.8 jit_solution(13398937736456145728)
XLA Ops:
  0.7 46.4 %shard_map.248 = (bf16[1,1,1,2816,128]{4,3,2,1,0:T(8,128)(2,1)S(1)}, f32[32,40,128]{2,1,0:T(8,128)S(1)}, f32[512,128]{1,0:T(8,128)S(1)}) custom-call(bf16[1,1,1,512,128]{4,3,2,1,0:T(8,128)(2,1)} %refs_0_.1, bf16[1,1,1,6,64,128]{5,4,3,2,1,0:T(8,128)(2,1)} %refs_1_.1, bf16[384,128]{1,0:T(8,128)(2,1)} %refs_2_.1, bf16[2,128,128]{2,1,0:T(8,128)(2,1)} %refs_3_.1, ...), custom_call_target="tpu_custom_call" | custom-call | flops 6000000000 | bytes 6000000 | tf_op jit(solution)/shard_map/pallas_call | solution.py:411
  47.1 1.8 %shard_map.249 = (bf16[1,1,1,2816,128]{4,3,2,1,0:T(8,128)(2,1)}, f32[1,1,1,512,128]{4,3,2,1,0:T(8,128)}, f32[384,128]{1,0:T(8,128)}, f32[2,128,128]{2,1,0:T(8,12...) custom-call(bf16[1,1,1,2816,128]{4,3,2,1,0:T(8,128)(2,1)S(1)} %get-t, ...), custom_call_target="tpu_custom_call" | custom-call | flops 1000000 | bytes 4000000 | tf_op jit(solution)/shard_map/pallas_call | solution.py:451

commit v3 on v2

--- a/solution.py
+++ b/solution.py
@@ -23,14 +23,16 @@
 RECV_TILES = NODES // D
 TILES = SEND_TILES + RECV_TILES
 PIECES = 32
-PIECE = 40
-ROW_EW1 = 0
-ROW_EWH = 384
-ROW_ESM = 640
-ROW_NW1 = 648
-ROW_NWH = 904
-ROW_NSM = 1160
-ROWS = PIECES * PIECE
+EDGE_PIECE = 21
+NODE_PIECE = 17
+EDGE_ROWS = PIECES * EDGE_PIECE
+NODE_ROWS = PIECES * NODE_PIECE
+ROW_EWH = 3 * D
+ROW_ESM = 5 * D
+ROW_NWH = 2 * D
+ROW_NSM = 4 * D
+
+
 PLANE_ORDER = (10, 9, 11, 6, 14, 2, 8, 5, 7, 13, 15, 1, 3, 4, 12)
 Z_ORDER = (4, 3, 5, 2, 6, 1, 7)
 
@@ -98,13 +100,8 @@
     return [jnp.where(hi == BF(k), base, zero) for k in range(tiles)]
 
 
-class Exchange:
-    def __init__(self, refs):
-        (
-            self.pack, self.pair_buf, self.half, self.plane_buf, self.zbuf, self.fin, self.gbuf,
-            self.pair_s, self.pair_r, self.plane_s, self.plane_r, self.z_s, self.z_r,
-            self.ag_s, self.ag_r, self.back_s, self.back_r, self.g_s, self.g_r,
-        ) = refs
+class Place:
+    def __init__(self):
         gx, gy, gz = lax.axis_index("gx"), lax.axis_index("gy"), lax.axis_index("gz")
         self.y, self.zl = gx // 2, gx % 2
         self.x, self.c = gz // 2, gz % 2
@@ -138,6 +135,9 @@
             pl.semaphore_signal(barrier, inc=1, device_id=peer, device_id_type=MESH)
         self.greeted = len(peers)
 
+    def meet(self):
+        pl.semaphore_wait(pltpu.get_barrier_semaphore(), self.greeted)
+
     def remote(self, src, dst, send, recv, peer):
         cp = pltpu.make_async_remote_copy(
             src_ref=src, dst_ref=dst, send_sem=send, recv_sem=recv, device_id=peer, device_id_type=MESH
@@ -146,92 +146,116 @@
         self.started.append(cp)
         return cp
 
-    def swap_halves(self):
-        pl.semaphore_wait(pltpu.get_barrier_semaphore(), self.greeted)
-        self.pair = self.remote(
-            self.pack.at[pl.ds((1 - self.c) * 16, 16)], self.pair_buf, self.pair_s, self.pair_r, self.sibling
-        )
-
-    def reduce_in_plane(self):
-        self.pair.wait_recv()
-        self.half[...] = self.pack[pl.ds(self.c * 16, 16)] + self.pair_buf[...]
-        self.in_plane = []
+    def drain(self):
+        for cp in self.started:
+            cp.wait_send()
+
+
+class AllReduce:
+    def __init__(self, place, piece, refs):
+        self.place, self.piece = place, piece
+        (
+            self.src, self.pair, self.half, self.inbox, self.zbuf, self.fin,
+            self.pair_s, self.pair_r, self.rs_s, self.rs_r, self.z_s, self.z_r,
+            self.ag_s, self.ag_r, self.back_s, self.back_r,
+        ) = refs
+
+    def swap_halves(self, pack_ref):
+        for p in range(PIECES):
+            self.src[p] = pack_ref[p * self.piece : (p + 1) * self.piece]
+        place = self.place
+        other = self.src.at[pl.ds((1 - place.c) * 16, 16)]
+        self.pending = [place.remote(other, self.pair, self.pair_s.at[0], self.pair_r.at[0], place.sibling)]
+
+    def arrived(self):
+        for cp in self.pending:
+            cp.wait_recv()
+
+    def in_plane(self):
+        place = self.place
+        self.arrived()
+        self.half[...] = self.src[pl.ds(place.c * 16, 16)] + self.pair[...]
+        self.pending = []
         for d in PLANE_ORDER:
-            index, peer = self.plane_peer(d)
-            self.in_plane.append(
-                self.remote(self.half.at[index], self.plane_buf.at[d], self.plane_s.at[d], self.plane_r.at[d], peer)
+            index, peer = place.plane_peer(d)
+            self.pending.append(
+                place.remote(self.half.at[index], self.inbox.at[d], self.rs_s.at[d], self.rs_r.at[d], peer)
             )
 
-    def send_ghosts(self, ghost_ref):
-        self.ghosts = [
-            self.remote(ghost_ref.at[f], self.gbuf.at[f], self.g_s.at[f], self.g_r.at[f], self.ghost_to[f])
-            for f in range(FACES)
+    def along_z(self):
+        self.arrived()
+        own = self.half[self.place.plane]
+        for d in range(1, 16):
+            own = own + self.inbox[d]
+        z = self.place.z
+        self.zbuf[z] = own
+        piece = self.zbuf.at[z]
+        self.pending = [
+            self.place.remote(piece, piece, self.z_s.at[d], self.z_r.at[d], self.place.z_peer(d)) for d in Z_ORDER
         ]
 
-    def reduce_along_z(self):
-        own = self.half[self.plane]
-        for cp in self.in_plane:
-            cp.wait_recv()
-        for d in range(1, 16):
-            own = own + self.plane_buf[d]
-        self.zbuf[self.z] = own
-        self.along_z = [
-            self.remote(self.zbuf.at[self.z], self.zbuf.at[self.z], self.z_s.at[d], self.z_r.at[d], self.z_peer(d))
-            for d in Z_ORDER
-        ]
-
-    def add_ghosts(self, total, rows_ref):
-        for f in range(FACES):
-            self.ghosts[f].wait_recv()
-            got = self.gbuf[f]
-            high = got.astype(BF)
-            low = (got - high.astype(F32)).astype(BF)
-            ids = jnp.broadcast_to(rows_ref[f], (NODES, SLOTS))
-            hot = jnp.where(ids == lax.broadcasted_iota(jnp.int32, (NODES, SLOTS), 0), 1.0, 0.0).astype(BF)
-            total = total + (mm(hot, high) + mm(hot, low))
-        return total
-
     def spread(self):
-        for cp in self.along_z:
-            cp.wait_recv()
+        place = self.place
+        self.arrived()
         own = self.zbuf[0]
         for d in range(1, 8):
             own = own + self.zbuf[d]
-        mine = self.c * 16 + self.plane
+        mine = place.c * 16 + place.plane
         self.fin[mine] = own
         piece = self.fin.at[mine]
-        gathers = [
-            self.remote(piece, piece, self.ag_s.at[d], self.ag_r.at[d], self.plane_peer(d)[1]) for d in PLANE_ORDER
+        self.pending = [
+            place.remote(piece, piece, self.ag_s.at[d], self.ag_r.at[d], place.plane_peer(d)[1]) for d in PLANE_ORDER
         ]
-        backs = [self.remote(piece, piece, self.back_s.at[0], self.back_r.at[0], self.sibling)]
-        for d, cp in reversed(list(zip(PLANE_ORDER, gathers))):
+        self.backs = [place.remote(piece, piece, self.back_s.at[0], self.back_r.at[0], place.sibling)]
+
+    def swap_back(self):
+        place = self.place
+        for d, cp in reversed(list(zip(PLANE_ORDER, self.pending))):
             cp.wait_recv()
             source = (4 - d // 4) % 4 * 4 + (4 - d % 4) % 4
-            piece = self.fin.at[self.c * 16 + self.plane_peer(source)[0]]
-            backs.append(self.remote(piece, piece, self.back_s.at[d], self.back_r.at[d], self.sibling))
-        for cp in backs:
-            cp.wait_recv()
-
-    def drain(self):
-        for cp in self.started:
-            cp.wait_send()
+            piece = self.fin.at[place.c * 16 + place.plane_peer(source)[0]]
+            self.backs.append(place.remote(piece, piece, self.back_s.at[d], self.back_r.at[d], place.sibling))
+        self.pending = self.backs
+
+    def finish(self, out_ref):
+        self.arrived()
+        for p in range(PIECES):
+            out_ref[p * self.piece : (p + 1) * self.piece] = self.fin[p]
+
+
+def send_ghosts(place, ghost_ref, gbuf, send, recv):
+    return [place.remote(ghost_ref.at[f], gbuf.at[f], send.at[f], recv.at[f], place.ghost_to[f]) for f in range(FACES)]
+
+
+def add_ghosts(total, copies, gbuf, rows_ref):
+    for f in range(FACES):
+        copies[f].wait_recv()
+        got = gbuf[f]
+        high = got.astype(BF)
+        low = (got - high.astype(F32)).astype(BF)
+        ids = jnp.broadcast_to(rows_ref[f], (NODES, SLOTS))
+        hot = jnp.where(ids == lax.broadcasted_iota(jnp.int32, (NODES, SLOTS), 0), 1.0, 0.0).astype(BF)
+        total = total + (mm(hot, high) + mm(hot, low))
+    return total
 
 
 def fused_kernel(scales, *refs):
     inputs, refs = refs[:INPUTS], refs[INPUTS:]
-    edge_out_ref, out_ref, node_out_ref = refs[:3]
-    held, refs = refs[3 : 3 + INPUTS], refs[3 + INPUTS :]
+    edge_out_ref, edge_sum_ref, node_sum_ref, node_out_ref = refs[:4]
+    held, refs = refs[4 : 4 + INPUTS], refs[4 + INPUTS :]
     in_sem = refs[0]
     (
         table, z1, z2, sl1, sl2, nrm, inv, rlo, rhi, agg, acc, w3t, w2t, w1t, aggb, small,
-        local_ref, ghost_out_ref, pack_ref,
-    ) = refs[1:20]
-    comm_refs = refs[20:]
+        local_ref, ghost_out_ref, pack_ref, node_pack_ref, full_t, g1b,
+    ) = refs[1:23]
+    edge_comm, node_comm, (gbuf, g_s, g_r) = refs[23:39], refs[39:55], refs[55:]
     loads = [pltpu.make_async_copy(a, b, in_sem.at[k]) for k, (a, b) in enumerate(zip(inputs, held))]
     for cp in loads:
         cp.start()
-    comm = Exchange(comm_refs)
-    comm.greet()
+    place = Place()
+    place.greet()
+    edge_reduce = AllReduce(place, EDGE_PIECE, edge_comm)
+    node_reduce = AllReduce(place, NODE_PIECE, node_comm)
     (
         node_ref, ghost_ref, ew1_ref, ewh_ref, send_ref, recv_ref, edge_ref, eb_ref, eg_ref, es_ref,
         nw1_ref, nwh_ref, nb_ref, ng_ref, ncot_ref, ecot_ref, rows_ref,
@@ -252,6 +276,7 @@
     acc[...] = jnp.zeros_like(acc)
     small[...] = jnp.zeros_like(small)
     pack_ref[...] = jnp.zeros_like(pack_ref)
+    node_pack_ref[ROW_NSM:] = jnp.zeros((NODE_ROWS - ROW_NSM, D), F32)
     for cp in loads[4:10]:
         cp.wait()
     egain = eg_ref[...].reshape(1, D)
@@ -307,16 +332,18 @@
     h1 = g1.astype(BF)
     local_ref[...] = u + mm(h1, transposed(nw1_ref[0:D]))
     aggb[...] = mm(h1, transposed(nw1_ref[D : 2 * D])).astype(BF)
-    pack_ref[ROW_NW1 : ROW_NW1 + 2 * D] = mm_tn(node_in, h1) * node_scale
-    pack_ref[ROW_NWH : ROW_NWH + D] = mm_tn(b1, h2) * node_scale
-    pack_ref[ROW_NWH + D : ROW_NWH + 2 * D] = mm_tn(b2, h3) * node_scale
-    pack_ref[ROW_NSM : ROW_NSM + 4] = node_scale * jnp.concatenate(
+    node_pack_ref[0 : 2 * D] = mm_tn(node_in, h1) * node_scale
+    node_pack_ref[ROW_NWH : ROW_NWH + D] = mm_tn(b1, h2) * node_scale
+    node_pack_ref[ROW_NWH + D : ROW_NWH + 2 * D] = mm_tn(b2, h3) * node_scale
+    node_pack_ref[ROW_NSM : ROW_NSM + 4] = node_scale * jnp.concatenate(
         [row_sum(g1), row_sum(g2), row_sum(g3), row_sum(u * n)], 0
     )
+    full_t[...] = full.astype(F32).T.astype(BF)
+    place.meet()
+    node_reduce.swap_halves(node_pack_ref)
 
     def backward(i, carry):
-        off = pl.multiple_of(i * CH, CH)
-        rows = pl.ds(off, CH)
+        rows = pl.ds(i * CH, CH)
         s_row = send_ref[0, 0, :, rows]
         r_row = recv_ref[0, 0, :, rows]
         hot = jnp.concatenate(one_hot_columns(rlo[rows], rhi[rows], RECV_TILES), 1)
@@ -329,8 +356,8 @@
         h2 = g2.astype(BF)
         g1 = mm(h2, w2t[...]) * sl1[rows]
         h1 = g1.astype(BF)
-        edge_out_ref[0, 0, 0, rows] = (cot + mm(h1, w1t[...])).astype(BF)
-        pack_ref[ROW_EW1 : ROW_EW1 + D] += mm_tn(edge_ref[0, 0, 0, rows], h1)
+        g1b[rows] = h1
+        pack_ref[0:D] += mm_tn(edge_ref[0, 0, 0, rows], h1)
         pack_ref[ROW_EWH : ROW_EWH + D] += mm_tn(z1[rows], h2)
         pack_ref[ROW_EWH + D : ROW_EWH + 2 * D] += mm_tn(z2[rows], h3)
         hot_t = jnp.concatenate(one_hot_rows(s_row, SEND_TILES) + one_hot_rows(r_row, RECV_TILES), 0)
@@ -342,30 +369,37 @@
         small[4] += fold(u)
         return carry
 
-    lax.fori_loop(0, CHUNKS, backward, 0)
+    for i in range(CHUNKS):
+        backward(i, 0)
+        if i == 0:
+            node_reduce.in_plane()
 
     sums = acc[0:FULL].astype(BF)
     sums_r = acc[FULL : FULL + NODES].astype(BF)
-    pack_ref[ROW_EW1 : ROW_EW1 + D] = pack_ref[ROW_EW1 : ROW_EW1 + D] * edge_scale
-    pack_ref[ROW_EW1 + D : ROW_EW1 + 2 * D] = mm_tn(full, sums) * edge_scale
-    pack_ref[ROW_EW1 + 2 * D : ROW_EW1 + 3 * D] = mm_tn(node, sums_r) * edge_scale
+    pack_ref[0:D] = pack_ref[0:D] * edge_scale
+    pack_ref[D : 2 * D] = mm(full_t[...], sums) * edge_scale
+    pack_ref[2 * D : 3 * D] = mm(full_t[:, 0:NODES], sums_r) * edge_scale
     pack_ref[ROW_EWH : ROW_EWH + 2 * D] = pack_ref[ROW_EWH : ROW_EWH + 2 * D] * edge_scale
     pack_ref[ROW_ESM : ROW_ESM + 5] = edge_scale * jnp.concatenate(
         [jnp.sum(small[j], 0, keepdims=True) for j in range(5)], 0
     )
-    for p in range(PIECES):
-        comm.pack[p] = pack_ref[p * PIECE : (p + 1) * PIECE]
-    comm.swap_halves()
+    edge_reduce.swap_halves(pack_ref)
     back = mm(sums, transposed(ew1_ref[D : 2 * D]))
+    ghost_out_ref[...] = back[NODES:].reshape(FACES, SLOTS, D)
+    node_reduce.along_z()
+    edge_reduce.in_plane()
+    ghosts = send_ghosts(place, ghost_out_ref, gbuf, g_s, g_r)
     local_ref[...] += back[0:NODES] + mm(sums_r, transposed(ew1_ref[2 * D : 3 * D]))
-    ghost_out_ref[...] = back[NODES:].reshape(FACES, SLOTS, D)
-    comm.reduce_in_plane()
-    comm.send_ghosts(ghost_out_ref)
-    comm.reduce_along_z()
-    node_out_ref[...] = comm.add_ghosts(local_ref[...], rows_ref)
-    comm.spread()
-    out_ref[...] = comm.fin[...]
-    comm.drain()
+    edge_out_ref[0, 0, 0] = (ecot_ref[0, 0, 0].astype(F32) + mm(g1b[...], w1t[...])).astype(BF)
+    node_reduce.spread()
+    edge_reduce.along_z()
+    node_out_ref[...] = add_ghosts(local_ref[...], ghosts, gbuf, rows_ref)
+    edge_reduce.spread()
+    node_reduce.swap_back()
+    edge_reduce.swap_back()
+    node_reduce.finish(node_sum_ref)
+    edge_reduce.finish(edge_sum_ref)
+    place.drain()
 
 
 VMEM = pl.BlockSpec(memory_space=pltpu.VMEM)
@@ -395,68 +429,78 @@
         pltpu.VMEM((5, 8, D), F32),
         pltpu.VMEM((NODES, D), F32),
         pltpu.VMEM((FACES, SLOTS, D), F32),
-        pltpu.VMEM((ROWS, D), F32),
-        pltpu.VMEM((PIECES, PIECE, D), F32),
-        pltpu.VMEM((16, PIECE, D), F32),
-        pltpu.VMEM((16, PIECE, D), F32),
-        pltpu.VMEM((16, PIECE, D), F32),
-        pltpu.VMEM((8, PIECE, D), F32),
-        pltpu.VMEM((PIECES, PIECE, D), F32),
+        pltpu.VMEM((EDGE_ROWS, D), F32),
+        pltpu.VMEM((NODE_ROWS, D), F32),
+        pltpu.VMEM((D, FULL), BF),
+        pltpu.VMEM((EDGES, D), BF),
+    ]
+    for piece in (EDGE_PIECE, NODE_PIECE):
+        scratch += [pltpu.VMEM((n, piece, D), F32) for n in (PIECES, 16, 16, 16, 8, PIECES)]
+        scratch += [pltpu.SemaphoreType.DMA((n,)) for n in (1, 1, 16, 16, 8, 8, 16, 16, 16, 16)]
+    scratch += [
         pltpu.VMEM((FACES, SLOTS, D), F32),
-        pltpu.SemaphoreType.DMA,
-        pltpu.SemaphoreType.DMA,
+        pltpu.SemaphoreType.DMA((FACES,)),
+        pltpu.SemaphoreType.DMA((FACES,)),
     ]
-    for n in (16, 16, 8, 8, 16, 16, 16, 16, FACES, FACES):
-        scratch.append(pltpu.SemaphoreType.DMA((n,)))
     return pl.pallas_call(
         functools.partial(fused_kernel, scales),
         out_shape=(
             jax.ShapeDtypeStruct((1, 1, 1, EDGES, D), BF),
-            jax.ShapeDtypeStruct((PIECES, PIECE, D), F32),
+            jax.ShapeDtypeStruct((EDGE_ROWS, D), F32),
+            jax.ShapeDtypeStruct((NODE_ROWS, D), F32),
             jax.ShapeDtypeStruct((NODES, D), F32),
         ),
         in_specs=[HBM] * INPUTS,
-        out_specs=(VMEM,) * 3,
+        out_specs=(VMEM,) * 4,
         scratch_shapes=scratch,
         compiler_params=pltpu.CompilerParams(collective_id=0, has_side_effects=True, vmem_limit_bytes=52 * 2**20),
         cost_estimate=pl.CostEstimate(flops=6_000_000_000, bytes_accessed=6_000_000, transcendentals=800_000),
     )(*[pltpu.with_memory_space_constraint(a, pltpu.HBM) for a in args])
 
 
-def unpack_kernel(edge_in, pack_in, node_in, edge_out, node_out, ew1, ewh, nw1, nwh, eb, eg, es, nb, ng, sem):
+def unpack_kernel(
+    edge_in, edge_sum, node_sum, node_in,
+    edge_out, node_out, ew1, ewh, nw1, nwh, eb, eg, es, nb, ng,
+    eb_v, eg_v, es_v, nb_v, ng_v, sem,
+):
+    eb_v[...] = edge_sum[ROW_ESM : ROW_ESM + 3]
+    eg_v[...] = edge_sum[ROW_ESM + 3 : ROW_ESM + 4].reshape(D)
+    es_v[...] = edge_sum[ROW_ESM + 4 : ROW_ESM + 5].reshape(D)
+    nb_v[...] = node_sum[ROW_NSM : ROW_NSM + 3]
+    ng_v[...] = node_sum[ROW_NSM + 3 : ROW_NSM + 4].reshape(D)
     moves = (
         (edge_in, edge_out),
         (node_in, node_out.at[0, 0, 0]),
-        (pack_in.at[ROW_EW1 : ROW_EW1 + 3 * D], ew1),
-        (pack_in.at[ROW_EWH : ROW_EWH + D], ewh.at[0]),
-        (pack_in.at[ROW_EWH + D : ROW_EWH + 2 * D], ewh.at[1]),
-        (pack_in.at[ROW_NW1 : ROW_NW1 + 2 * D], nw1),
-        (pack_in.at[ROW_NWH : ROW_NWH + D], nwh.at[0]),
-        (pack_in.at[ROW_NWH + D : ROW_NWH + 2 * D], nwh.at[1]),
+        (edge_sum.at[0 : 3 * D], ew1),
+        (edge_sum.at[ROW_EWH : ROW_EWH + D], ewh.at[0]),
+        (edge_sum.at[ROW_EWH + D : ROW_EWH + 2 * D], ewh.at[1]),
+        (node_sum.at[0 : 2 * D], nw1),
+        (node_sum.at[ROW_NWH : ROW_NWH + D], nwh.at[0]),
+        (node_sum.at[ROW_NWH + D : ROW_NWH + 2 * D], nwh.at[1]),
+        (eb_v, eb),
+        (eg_v, eg),
+        (es_v, es),
+        (nb_v, nb),
+        (ng_v, ng),
     )
     copies = [pltpu.make_async_copy(a, b, sem.at[k]) for k, (a, b) in enumerate(moves)]
     for cp in copies:
         cp.start()
-    eb[...] = pack_in[ROW_ESM : ROW_ESM + 3]
-    eg[...] = pack_in[ROW_ESM + 3 : ROW_ESM + 4].reshape(D)
-    es[...] = pack_in[ROW_ESM + 4 : ROW_ESM + 5].reshape(D)
-    nb[...] = pack_in[ROW_NSM : ROW_NSM + 3]
-    ng[...] = pack_in[ROW_NSM + 3 : ROW_NSM + 4].reshape(D)
     for cp in copies:
         cp.wait()
 
 
-def unpack(edge, pack, node):
+def unpack(edge, edge_sum, node_sum, node):
     shapes = ((1, 1, 1, NODES, D), (3 * D, D), (2, D, D), (2 * D, D), (2, D, D), (3, D), (D,), (D,), (3, D), (D,))
     return pl.pallas_call(
         unpack_kernel,
         out_shape=(jax.ShapeDtypeStruct(edge.shape, BF),) + tuple(jax.ShapeDtypeStruct(s, F32) for s in shapes),
-        in_specs=[VMEM] * 3,
-        out_specs=(HBM,) * 6 + (VMEM,) * 5,
-        scratch_shapes=[pltpu.SemaphoreType.DMA((8,))],
+        in_specs=[VMEM] * 4,
+        out_specs=(HBM,) * 11,
+        scratch_shapes=[pltpu.VMEM(s, F32) for s in shapes[5:]] + [pltpu.SemaphoreType.DMA((13,))],
         compiler_params=pltpu.CompilerParams(vmem_limit_bytes=8 * 2**20),
         cost_estimate=pl.CostEstimate(flops=1_000_000, bytes_accessed=4_000_000, transcendentals=0),
-    )(edge, pack, node)
+    )(edge, edge_sum, node_sum, node)
 
 
 def on_device(
@@ -465,7 +509,7 @@
 ):
     devices = lax.axis_size("gx") * lax.axis_size("gy") * lax.axis_size("gz")
     scales = (float(EDGES * devices) ** (-0.5), float(NODES * devices) ** (-0.5))
-    edge, summed, node = fused(
+    edge, edge_sum, node_sum, node = fused(
         (
             node_latent, ghost_latent, w_edge_in, w_edge_hidden, senders, receivers, edge_latent,
             b_edge, gain_edge, shift_edge, w_node_in, w_node_hidden, b_node, gain_node,
@@ -473,7 +517,7 @@
         ),
         scales,
     )
-    edge_grad, node_grad, ew1, ewh, nw1, nwh, eb, eg, es, nb, ng = unpack(edge, summed.reshape(ROWS, D), node)
+    edge_grad, node_grad, ew1, ewh, nw1, nwh, eb, eg, es, nb, ng = unpack(edge, edge_sum, node_sum, node)
     return (node_grad, edge_grad, ew1, ewh, eb, eg, es, nw1, nwh, nb, ng)
 
 

time: 48.9 us -> 46.1 us (0.943)
  Pallas kernels: 48.2 us -> 45.1 us
    pallas_call x1, Pallas kernels: 46.4 us -> 43.9 us  [fused(): pl.pallas_call(functools.partial(fused_kernel, scales), out_shape=(jax.Sh...]
    pallas_call x1, Pallas kernels: 1.79 us -> 1.25 us  [unpack(): pl.pallas_call(unpack_kernel, out_shape=(jax.ShapeDtypeStruct(edge.shape,...]
where the time goes in v3:
time: 46.1 us; the launch traced here: 46 us
  Pallas kernels  45.1 us (98%)
  between operations  0.82 us (2%)
    pallas_call x1, Pallas kernels, fused(): pl.pallas_call(functools.partial(fused_kernel, scales), out_shape=(jax.Sh...  43.9 us
    pallas_call x1, Pallas kernels, unpack(): pl.pallas_call(unpack_kernel, out_shape=(jax.ShapeDtypeStruct(edge.shape,...  1.25 us

profile of v3, /device:TPU:1, one launch (start us, length us, event | category | flops | bytes accessed | tf_op | source)
XLA Modules:
  0.0 46.0 jit_solution(6507854443421590219)
XLA Ops:
  0.7 43.9 %shard_map.248 = (bf16[1,1,1,2816,128]{4,3,2,1,0:T(8,128)(2,1)S(1)}, f32[672,128]{1,0:T(8,128)S(1)}, f32[544,128]{1,0:T(8,128)S(1)}, f32[512,128]{1,0:T(8,128)S(1)}) custom-call(bf16[1,1,1,512,128]{4,3,2,1,0:T(8,128)(2,1)} %refs_0_.1, bf16[1,1,1,6,64,128]{5,4,3,2,1,0:T(8,128)(2,1)} %refs_1_.1, bf16[384,128]{1,0:T(8,128)(2,1)} %refs_2_.1, ...), custom_call_target="tpu_custom_call" | custom-call | flops 6000000000 | bytes 6000000 | tf_op jit(solution)/shard_map/pallas_call | solution.py:445
  44.5 1.3 %shard_map.249 = (bf16[1,1,1,2816,128]{4,3,2,1,0:T(8,128)(2,1)}, f32[1,1,1,512,128]{4,3,2,1,0:T(8,128)}, f32[384,128]{1,0:T(8,128)}, f32[2,128,128]{2,1,0:T(8,12...) custom-call(bf16[1,1,1,2816,128]{4,3,2,1,0:T(8,128)(2,1)S(1)} %get-t, ...), custom_call_target="tpu_custom_call" | custom-call | flops 1000000 | bytes 4000000 | tf_op jit(solution)/shard_map/pallas_call | solution.py:495

commit v4 on v3

--- a/solution.py
+++ b/solution.py
@@ -45,6 +45,10 @@
     return lax.dot_general(a, b, (((0,), (0,)), ((), ())), preferred_element_type=F32)
 
 
+def mm_nt(a, b):
+    return lax.dot_general(a, b, (((1,), (1,)), ((), ())), preferred_element_type=F32)
+
+
 def transposed(w):
     return w.astype(F32).T.astype(BF)
 
@@ -56,31 +60,39 @@
 
 
 def norm_parts(p):
-    c = p - jnp.mean(p, -1, keepdims=True)
-    inv = lax.rsqrt(jnp.mean(c * c, -1, keepdims=True) + EPSILON)
+    c = p - jnp.mean(p, 0, keepdims=True)
+    inv = lax.rsqrt(jnp.mean(c * c, 0, keepdims=True) + EPSILON)
     return c * inv, inv
 
 
 def norm_back(u, gain, n, inv):
     t = u * gain
-    return inv * (t - jnp.mean(t, -1, keepdims=True) - n * jnp.mean(t * n, -1, keepdims=True))
+    return inv * (t - jnp.mean(t, 0, keepdims=True) - n * jnp.mean(t * n, 0, keepdims=True))
+
+
+def wide(column, n):
+    return jnp.concatenate([column] * (n // D), 1)
 
 
 def fold(x):
-    return jnp.sum(x.reshape(x.shape[0] // 8, 8, x.shape[1]), 0)
-
-
-def row_sum(x):
-    return jnp.sum(fold(x), 0, keepdims=True)
-
-
-def column_digits(ids_row):
-    lo, hi = [], []
-    for j in range(ids_row.shape[1] // D):
-        t = jnp.broadcast_to(ids_row[:, j * D : (j + 1) * D], (D, D)).T
-        lo.append((t & (D - 1)).astype(F32).astype(BF))
-        hi.append((t >> 7).astype(F32).astype(BF))
-    return jnp.concatenate(lo, 0), jnp.concatenate(hi, 0)
+    total = x[:, 0:D]
+    for k in range(1, x.shape[1] // D):
+        total = total + x[:, k * D : (k + 1) * D]
+    return total
+
+
+def lane_sum(x):
+    return jnp.sum(x.T, 0, keepdims=True)
+
+
+def column_digits(s_row, r_row):
+    both = s_row + (r_row << 10)
+    parts = []
+    for j in range(both.shape[1] // D):
+        t = jnp.broadcast_to(both[:, j * D : (j + 1) * D], (D, D)).T
+        digits = (t & (D - 1), (t >> 7) & 7, (t >> 10) & (D - 1), t >> 17)
+        parts.append([d.astype(F32).astype(BF) for d in digits])
+    return [jnp.concatenate(p, 0) for p in zip(*parts)]
 
 
 def one_hot_columns(lo, hi, tiles):
@@ -245,10 +257,10 @@
     held, refs = refs[4 : 4 + INPUTS], refs[4 + INPUTS :]
     in_sem = refs[0]
     (
-        table, z1, z2, sl1, sl2, nrm, inv, rlo, rhi, agg, acc, w3t, w2t, w1t, aggb, small,
-        local_ref, ghost_out_ref, pack_ref, node_pack_ref, full_t, g1b,
-    ) = refs[1:23]
-    edge_comm, node_comm, (gbuf, g_s, g_r) = refs[23:39], refs[39:55], refs[55:]
+        table_t, full_t, z1, z2, sl1, sl2, nrm, inv, slo, shi, rlo, rhi, g1b, agg, acc, aggb, small, cols,
+        w2t, w3t, node_h1, local_ref, ghost_out_ref, pack_ref, node_pack_ref,
+    ) = refs[1:26]
+    edge_comm, node_comm, (gbuf, g_s, g_r) = refs[26:42], refs[42:58], refs[58:]
     loads = [pltpu.make_async_copy(a, b, in_sem.at[k]) for k, (a, b) in enumerate(zip(inputs, held))]
     for cp in loads:
         cp.start()
@@ -263,134 +275,143 @@
     edge_scale, node_scale = scales
     for cp in loads[:4]:
         cp.wait()
-    node = node_ref[0, 0, 0]
     ghosts = ghost_ref[0, 0, 0].reshape(FACES * SLOTS, D)
-    full = jnp.concatenate([node, ghosts], 0)
-    table[0:FULL] = mm(full, ew1_ref[D : 2 * D]).astype(BF)
-    table[FULL : FULL + NODES] = mm(node, ew1_ref[2 * D : 3 * D]).astype(BF)
-    table[FULL + NODES :] = ew1_ref[0:D]
+    full_t[...] = jnp.concatenate([transposed(node_ref[0, 0, 0]), transposed(ghosts)], 1)
+    table_t[:, 0:FULL] = mm(transposed(ew1_ref[D : 2 * D]), full_t[...]).astype(BF)
+    table_t[:, FULL : FULL + NODES] = mm(transposed(ew1_ref[2 * D : 3 * D]), full_t[:, 0:NODES]).astype(BF)
+    table_t[:, FULL + NODES :] = transposed(ew1_ref[0:D])
+    w2t[...] = transposed(ewh_ref[0])
     w3t[...] = transposed(ewh_ref[1])
-    w2t[...] = transposed(ewh_ref[0])
-    w1t[...] = transposed(ew1_ref[0:D])
-    agg[...] = jnp.zeros_like(agg)
-    acc[...] = jnp.zeros_like(acc)
-    small[...] = jnp.zeros_like(small)
-    pack_ref[...] = jnp.zeros_like(pack_ref)
     node_pack_ref[ROW_NSM:] = jnp.zeros((NODE_ROWS - ROW_NSM, D), F32)
-    for cp in loads[4:10]:
+    pack_ref[ROW_ESM:] = jnp.zeros((EDGE_ROWS - ROW_ESM, D), F32)
+    for cp in loads[4:14]:
         cp.wait()
-    egain = eg_ref[...].reshape(1, D)
-    eshift = es_ref[...].reshape(1, D)
+    columns = [eb_ref[k : k + 1] for k in range(3)] + [eg_ref[...].reshape(1, D), es_ref[...].reshape(1, D)]
+    columns += [nb_ref[k : k + 1] for k in range(3)] + [ng_ref[...].reshape(1, D)]
+    for k, column in enumerate(columns):
+        cols[k] = jnp.broadcast_to(column, (D, D)).T
 
     def forward(i, carry):
         off = pl.multiple_of(i * CH, CH)
-        rows = pl.ds(off, CH)
-        s_row = send_ref[0, 0, :, rows]
-        r_row = recv_ref[0, 0, :, rows]
-        slo, shi = column_digits(s_row)
-        lo, hi = column_digits(r_row)
-        rlo[rows] = lo
-        rhi[rows] = hi
-        hot = one_hot_columns(slo, shi, SEND_TILES) + one_hot_columns(lo, hi, RECV_TILES)
-        lhs = jnp.concatenate(hot + [edge_ref[0, 0, 0, rows]], 1)
-        p1 = mm(lhs, table[...]) + eb_ref[0:1]
+        at = pl.ds(off, CH)
+        s_row = send_ref[0, 0, :, at]
+        r_row = recv_ref[0, 0, :, at]
+        hot = one_hot_rows(s_row, SEND_TILES) + one_hot_rows(r_row, RECV_TILES)
+        rhs = jnp.concatenate(hot + [transposed(edge_ref[0, 0, 0, at])], 0)
+        p1 = mm(table_t[...], rhs) + wide(cols[0], CH)
         a1, d1 = silu_parts(p1)
         b1 = a1.astype(BF)
-        z1[rows] = b1
-        sl1[rows] = d1
-        p2 = mm(b1, ewh_ref[0]) + eb_ref[1:2]
+        z1[i] = b1
+        sl1[i] = d1
+        p2 = mm(w2t[...], b1) + wide(cols[1], CH)
         a2, d2 = silu_parts(p2)
         b2 = a2.astype(BF)
-        z2[rows] = b2
-        sl2[rows] = d2
-        q = mm(b2, ewh_ref[1]) + eb_ref[2:3]
+        z2[i] = b2
+        sl2[i] = d2
+        q = mm(w3t[...], b2) + wide(cols[2], CH)
         n, iv = norm_parts(q)
-        nrm[rows] = n
-        inv[rows] = jnp.broadcast_to(iv, (CH, D))
-        new = (n * egain + eshift).astype(BF)
-        hot_t = jnp.concatenate(one_hot_rows(r_row, RECV_TILES), 0)
-        agg[...] += mm(hot_t, new)
+        nrm[i] = n
+        inv[i] = iv
+        new = (n * wide(cols[3], CH) + wide(cols[4], CH)).astype(BF)
+        slo[at], shi[at], lo, hi = column_digits(s_row, r_row)
+        rlo[at], rhi[at] = lo, hi
+        part = mm(new, jnp.concatenate(one_hot_columns(lo, hi, RECV_TILES), 1))
+
+        @pl.when(i == 0)
+        def _():
+            agg[...] = part
+
+        @pl.when(i > 0)
+        def _():
+            agg[...] += part
+
         return carry
 
     lax.fori_loop(0, CHUNKS, forward, 0)
 
-    for cp in loads[10:]:
+    for cp in loads[14:]:
         cp.wait()
-    ngain = ng_ref[...].reshape(1, D)
-    node_in = jnp.concatenate([node, agg[...].astype(BF)], 1)
-    a1, d1 = silu_parts(mm(node_in, nw1_ref[...]) + nb_ref[0:1])
+    node_in = jnp.concatenate([full_t[:, 0:NODES], agg[...].astype(BF)], 0)
+    a1, d1 = silu_parts(mm(transposed(nw1_ref[...]), node_in) + wide(cols[5], NODES))
     b1 = a1.astype(BF)
-    a2, d2 = silu_parts(mm(b1, nwh_ref[0]) + nb_ref[1:2])
+    a2, d2 = silu_parts(mm(transposed(nwh_ref[0]), b1) + wide(cols[6], NODES))
     b2 = a2.astype(BF)
-    n, iv = norm_parts(mm(b2, nwh_ref[1]) + nb_ref[2:3])
-    u = ncot_ref[0, 0, 0].astype(F32)
-    g3 = norm_back(u, ngain, n, iv)
+    n, iv = norm_parts(mm(transposed(nwh_ref[1]), b2) + wide(cols[7], NODES))
+    u = transposed(ncot_ref[0, 0, 0]).astype(F32)
+    g3 = norm_back(u, wide(cols[8], NODES), n, iv)
     h3 = g3.astype(BF)
-    g2 = mm(h3, transposed(nwh_ref[1])) * d2
+    g2 = mm(nwh_ref[1], h3) * d2
     h2 = g2.astype(BF)
-    g1 = mm(h2, transposed(nwh_ref[0])) * d1
+    g1 = mm(nwh_ref[0], h2) * d1
     h1 = g1.astype(BF)
-    local_ref[...] = u + mm(h1, transposed(nw1_ref[0:D]))
-    aggb[...] = mm(h1, transposed(nw1_ref[D : 2 * D])).astype(BF)
-    node_pack_ref[0 : 2 * D] = mm_tn(node_in, h1) * node_scale
-    node_pack_ref[ROW_NWH : ROW_NWH + D] = mm_tn(b1, h2) * node_scale
-    node_pack_ref[ROW_NWH + D : ROW_NWH + 2 * D] = mm_tn(b2, h3) * node_scale
+    node_h1[...] = h1
+    aggb[...] = mm(nw1_ref[D : 2 * D], h1).astype(BF)
+    node_pack_ref[0 : 2 * D] = mm_nt(node_in, h1) * node_scale
+    node_pack_ref[ROW_NWH : ROW_NWH + D] = mm_nt(b1, h2) * node_scale
+    node_pack_ref[ROW_NWH + D : ROW_NWH + 2 * D] = mm_nt(b2, h3) * node_scale
     node_pack_ref[ROW_NSM : ROW_NSM + 4] = node_scale * jnp.concatenate(
-        [row_sum(g1), row_sum(g2), row_sum(g3), row_sum(u * n)], 0
+        [lane_sum(fold(g1)), lane_sum(fold(g2)), lane_sum(fold(g3)), lane_sum(fold(u * n))], 0
     )
-    full_t[...] = full.astype(F32).T.astype(BF)
     place.meet()
     node_reduce.swap_halves(node_pack_ref)
 
-    def backward(i, carry):
-        rows = pl.ds(i * CH, CH)
-        s_row = send_ref[0, 0, :, rows]
-        r_row = recv_ref[0, 0, :, rows]
-        hot = jnp.concatenate(one_hot_columns(rlo[rows], rhi[rows], RECV_TILES), 1)
-        cot = ecot_ref[0, 0, 0, rows].astype(F32)
-        u = cot + mm(hot, aggb[...])
-        n = nrm[rows]
-        g3 = norm_back(u, egain, n, inv[rows])
+    def backward(i):
+        at = pl.ds(i * CH, CH)
+        first = i == 0
+
+        def add(ref, where, value):
+            if first:
+                ref[where] = value
+            else:
+                ref[where] += value
+
+        r_row = recv_ref[0, 0, :, at]
+        cot = transposed(ecot_ref[0, 0, 0, at]).astype(F32)
+        u = cot + mm(aggb[...], jnp.concatenate(one_hot_rows(r_row, RECV_TILES), 0))
+        n = nrm[i]
+        g3 = norm_back(u, wide(cols[3], CH), n, inv[i])
         h3 = g3.astype(BF)
-        g2 = mm(h3, w3t[...]) * sl2[rows]
+        g2 = mm(ewh_ref[1], h3) * sl2[i]
         h2 = g2.astype(BF)
-        g1 = mm(h2, w2t[...]) * sl1[rows]
+        g1 = mm(ewh_ref[0], h2) * sl1[i]
         h1 = g1.astype(BF)
-        g1b[rows] = h1
-        pack_ref[0:D] += mm_tn(edge_ref[0, 0, 0, rows], h1)
-        pack_ref[ROW_EWH : ROW_EWH + D] += mm_tn(z1[rows], h2)
-        pack_ref[ROW_EWH + D : ROW_EWH + 2 * D] += mm_tn(z2[rows], h3)
-        hot_t = jnp.concatenate(one_hot_rows(s_row, SEND_TILES) + one_hot_rows(r_row, RECV_TILES), 0)
-        acc[...] += mm(hot_t, h1)
-        small[0] += fold(g1)
-        small[1] += fold(g2)
-        small[2] += fold(g3)
-        small[3] += fold(u * n)
-        small[4] += fold(u)
-        return carry
+        g1b[i] = h1
+        add(pack_ref, pl.ds(ROW_EWH, D), mm_nt(z1[i], h2))
+        add(pack_ref, pl.ds(ROW_EWH + D, D), mm_nt(z2[i], h3))
+        hot = one_hot_columns(slo[at], shi[at], SEND_TILES) + one_hot_columns(rlo[at], rhi[at], RECV_TILES)
+        add(acc, slice(None), mm(h1, jnp.concatenate(hot + [edge_ref[0, 0, 0, at]], 1)))
+        for k, x in enumerate((g1, g2, g3, u * n, u)):
+            add(small, k, fold(x))
 
     for i in range(CHUNKS):
-        backward(i, 0)
+        backward(i)
         if i == 0:
             node_reduce.in_plane()
 
-    sums = acc[0:FULL].astype(BF)
-    sums_r = acc[FULL : FULL + NODES].astype(BF)
-    pack_ref[0:D] = pack_ref[0:D] * edge_scale
-    pack_ref[D : 2 * D] = mm(full_t[...], sums) * edge_scale
-    pack_ref[2 * D : 3 * D] = mm(full_t[:, 0:NODES], sums_r) * edge_scale
+    sums = acc[:, 0:FULL].astype(BF)
+    sums_r = acc[:, FULL : FULL + NODES].astype(BF)
+    pack_ref[0:D] = acc[:, FULL + NODES :].T * edge_scale
+    pack_ref[D : 2 * D] = mm_nt(full_t[...], sums) * edge_scale
+    pack_ref[2 * D : 3 * D] = mm_nt(full_t[:, 0:NODES], sums_r) * edge_scale
     pack_ref[ROW_EWH : ROW_EWH + 2 * D] = pack_ref[ROW_EWH : ROW_EWH + 2 * D] * edge_scale
-    pack_ref[ROW_ESM : ROW_ESM + 5] = edge_scale * jnp.concatenate(
-        [jnp.sum(small[j], 0, keepdims=True) for j in range(5)], 0
-    )
+    pack_ref[ROW_ESM : ROW_ESM + 5] = edge_scale * jnp.concatenate([lane_sum(small[j]) for j in range(5)], 0)
     edge_reduce.swap_halves(pack_ref)
-    back = mm(sums, transposed(ew1_ref[D : 2 * D]))
+    back = mm_tn(sums, transposed(ew1_ref[D : 2 * D]))
     ghost_out_ref[...] = back[NODES:].reshape(FACES, SLOTS, D)
     node_reduce.along_z()
     edge_reduce.in_plane()
     ghosts = send_ghosts(place, ghost_out_ref, gbuf, g_s, g_r)
-    local_ref[...] += back[0:NODES] + mm(sums_r, transposed(ew1_ref[2 * D : 3 * D]))
-    edge_out_ref[0, 0, 0] = (ecot_ref[0, 0, 0].astype(F32) + mm(g1b[...], w1t[...])).astype(BF)
+    local_ref[...] = (
+        ncot_ref[0, 0, 0].astype(F32)
+        + mm_tn(node_h1[...], transposed(nw1_ref[0:D]))
+        + back[0:NODES]
+        + mm_tn(sums_r, transposed(ew1_ref[2 * D : 3 * D]))
+    )
+    for i in range(CHUNKS):
+        at = pl.ds(i * CH, CH)
+        edge_out_ref[0, 0, 0, at] = (
+            ecot_ref[0, 0, 0, at].astype(F32) + mm_tn(g1b[i], transposed(ew1_ref[0:D]))
+        ).astype(BF)
     node_reduce.spread()
     edge_reduce.along_z()
     node_out_ref[...] = add_ghosts(local_ref[...], ghosts, gbuf, rows_ref)
@@ -411,28 +432,31 @@
     scratch = [pltpu.VMEM(a.shape, a.dtype) for a in args]
     scratch += [
         pltpu.SemaphoreType.DMA((INPUTS,)),
-        pltpu.VMEM((FULL + NODES + D, D), BF),
+        pltpu.VMEM((D, FULL + NODES + D), BF),
+        pltpu.VMEM((D, FULL), BF),
+        pltpu.VMEM((CHUNKS, D, CH), BF),
+        pltpu.VMEM((CHUNKS, D, CH), BF),
+        pltpu.VMEM((CHUNKS, D, CH), F32),
+        pltpu.VMEM((CHUNKS, D, CH), F32),
+        pltpu.VMEM((CHUNKS, D, CH), F32),
+        pltpu.VMEM((CHUNKS, 1, CH), F32),
         pltpu.VMEM((EDGES, D), BF),
         pltpu.VMEM((EDGES, D), BF),
-        pltpu.VMEM((EDGES, D), F32),
-        pltpu.VMEM((EDGES, D), F32),
-        pltpu.VMEM((EDGES, D), F32),
-        pltpu.VMEM((EDGES, D), F32),
         pltpu.VMEM((EDGES, D), BF),
         pltpu.VMEM((EDGES, D), BF),
-        pltpu.VMEM((NODES, D), F32),
-        pltpu.VMEM((FULL + NODES, D), F32),
+        pltpu.VMEM((CHUNKS, D, CH), BF),
+        pltpu.VMEM((D, NODES), F32),
+        pltpu.VMEM((D, FULL + NODES + D), F32),
+        pltpu.VMEM((D, NODES), BF),
+        pltpu.VMEM((5, D, D), F32),
+        pltpu.VMEM((9, D, D), F32),
         pltpu.VMEM((D, D), BF),
         pltpu.VMEM((D, D), BF),
-        pltpu.VMEM((D, D), BF),
-        pltpu.VMEM((NODES, D), BF),
-        pltpu.VMEM((5, 8, D), F32),
+        pltpu.VMEM((D, NODES), BF),
         pltpu.VMEM((NODES, D), F32),
         pltpu.VMEM((FACES, SLOTS, D), F32),
         pltpu.VMEM((EDGE_ROWS, D), F32),
         pltpu.VMEM((NODE_ROWS, D), F32),
-        pltpu.VMEM((D, FULL), BF),
-        pltpu.VMEM((EDGES, D), BF),
     ]
     for piece in (EDGE_PIECE, NODE_PIECE):
         scratch += [pltpu.VMEM((n, piece, D), F32) for n in (PIECES, 16, 16, 16, 8, PIECES)]

time: 46.1 us -> 42.4 us (0.920)
  Pallas kernels: 45.1 us -> 41.7 us
    pallas_call x1, Pallas kernels: 43.9 us -> 40.4 us  [fused(): pl.pallas_call(functools.partial(fused_kernel, scales), out_shape=(jax.Sh...]
where the time goes in v4:
time: 42.4 us; the launch traced here: 42.3 us
  Pallas kernels  41.7 us (98%)
  between operations  0.66 us (2%)
    pallas_call x1, Pallas kernels, fused(): pl.pallas_call(functools.partial(fused_kernel, scales), out_shape=(jax.Sh...  40.4 us
    pallas_call x1, Pallas kernels, unpack(): pl.pallas_call(unpack_kernel, out_shape=(jax.ShapeDtypeStruct(edge.shape,...  1.25 us

profile of v4, /device:TPU:1, one launch (start us, length us, event | category | flops | bytes accessed | tf_op | source)
XLA Modules:
  0.0 42.3 jit_solution(18061789161930899749)
XLA Ops:
  0.7 40.4 %shard_map.248 = (bf16[1,1,1,2816,128]{4,3,2,1,0:T(8,128)(2,1)S(1)}, f32[672,128]{1,0:T(8,128)S(1)}, f32[544,128]{1,0:T(8,128)S(1)}, f32[512,128]{1,0:T(8,128)S(1)}) custom-call(bf16[1,1,1,512,128]{4,3,2,1,0:T(8,128)(2,1)} %refs_0_.1, bf16[1,1,1,6,64,128]{5,4,3,2,1,0:T(8,128)(2,1)} %refs_1_.1, bf16[384,128]{1,0:T(8,128)(2,1)} %refs_2_.1, ...), custom_call_target="tpu_custom_call" | custom-call | flops 6000000000 | bytes 6000000 | tf_op jit(solution)/shard_map/pallas_call | solution.py:469
  41.1 1.3 %shard_map.249 = (bf16[1,1,1,2816,128]{4,3,2,1,0:T(8,128)(2,1)}, f32[1,1,1,512,128]{4,3,2,1,0:T(8,128)}, f32[384,128]{1,0:T(8,128)}, f32[2,128,128]{2,1,0:T(8,12...) custom-call(bf16[1,1,1,2816,128]{4,3,2,1,0:T(8,128)(2,1)S(1)} %get-t, ...), custom_call_target="tpu_custom_call" | custom-call | flops 1000000 | bytes 4000000 | tf_op jit(solution)/shard_map/pallas_call | solution.py:519

commit v5 on v4

--- a/solution.py
+++ b/solution.py
@@ -50,13 +50,17 @@
 
 
 def transposed(w):
-    return w.astype(F32).T.astype(BF)
-
-
-def silu_parts(p):
-    s = 0.5 * jnp.tanh(0.5 * p) + 0.5
-    z = p * s
-    return z, s + z * (1.0 - s)
+    return w.T
+
+
+def halved(w):
+    return (w.astype(F32) * 0.5).astype(BF)
+
+
+def silu_parts(h):
+    t = jnp.tanh(h)
+    z = h + h * t
+    return z, (1.0 + t) + z * (1.0 - t)
 
 
 def norm_parts(p):
@@ -85,14 +89,15 @@
     return jnp.sum(x.T, 0, keepdims=True)
 
 
-def column_digits(s_row, r_row):
-    both = s_row + (r_row << 10)
+def column_digits(ids_row):
     parts = []
-    for j in range(both.shape[1] // D):
-        t = jnp.broadcast_to(both[:, j * D : (j + 1) * D], (D, D)).T
-        digits = (t & (D - 1), (t >> 7) & 7, (t >> 10) & (D - 1), t >> 17)
-        parts.append([d.astype(F32).astype(BF) for d in digits])
-    return [jnp.concatenate(p, 0) for p in zip(*parts)]
+    for digit in (ids_row & (D - 1), ids_row >> 7):
+        row = digit.astype(F32)
+        tiles = [
+            jnp.broadcast_to(row[:, j : j + D], (D, D)).astype(BF).T for j in range(0, ids_row.shape[1], D)
+        ]
+        parts.append(jnp.concatenate(tiles, 0))
+    return parts
 
 
 def one_hot_columns(lo, hi, tiles):
@@ -257,10 +262,10 @@
     held, refs = refs[4 : 4 + INPUTS], refs[4 + INPUTS :]
     in_sem = refs[0]
     (
-        table_t, full_t, z1, z2, sl1, sl2, nrm, inv, slo, shi, rlo, rhi, g1b, agg, acc, aggb, small, cols,
-        w2t, w3t, node_h1, local_ref, ghost_out_ref, pack_ref, node_pack_ref,
-    ) = refs[1:26]
-    edge_comm, node_comm, (gbuf, g_s, g_r) = refs[26:42], refs[42:58], refs[58:]
+        table_t, full_t, z1, z2, sl1, sl2, nrm, inv, slo, shi, to_rows, to_cols, g1b, agg, acc, aggb, small, cols,
+        w2t, w3t, w2h, w3h, node_h1, local_ref, ghost_out_ref, pack_ref, node_pack_ref,
+    ) = refs[1:28]
+    edge_comm, node_comm, (gbuf, g_s, g_r) = refs[28:44], refs[44:60], refs[60:]
     loads = [pltpu.make_async_copy(a, b, in_sem.at[k]) for k, (a, b) in enumerate(zip(inputs, held))]
     for cp in loads:
         cp.start()
@@ -277,28 +282,34 @@
         cp.wait()
     ghosts = ghost_ref[0, 0, 0].reshape(FACES * SLOTS, D)
     full_t[...] = jnp.concatenate([transposed(node_ref[0, 0, 0]), transposed(ghosts)], 1)
-    table_t[:, 0:FULL] = mm(transposed(ew1_ref[D : 2 * D]), full_t[...]).astype(BF)
-    table_t[:, FULL : FULL + NODES] = mm(transposed(ew1_ref[2 * D : 3 * D]), full_t[:, 0:NODES]).astype(BF)
-    table_t[:, FULL + NODES :] = transposed(ew1_ref[0:D])
-    w2t[...] = transposed(ewh_ref[0])
+    table_t[:, 0:FULL] = mm(halved(transposed(ew1_ref[D : 2 * D])), full_t[...]).astype(BF)
+    table_t[:, FULL + NODES :] = halved(transposed(ew1_ref[0:D]))
+    w2t[...] = halved(transposed(ewh_ref[0]))
     w3t[...] = transposed(ewh_ref[1])
+    w2h[...] = halved(ewh_ref[0])
+    w3h[...] = halved(ewh_ref[1])
     node_pack_ref[ROW_NSM:] = jnp.zeros((NODE_ROWS - ROW_NSM, D), F32)
     pack_ref[ROW_ESM:] = jnp.zeros((EDGE_ROWS - ROW_ESM, D), F32)
     for cp in loads[4:14]:
         cp.wait()
     columns = [eb_ref[k : k + 1] for k in range(3)] + [eg_ref[...].reshape(1, D), es_ref[...].reshape(1, D)]
     columns += [nb_ref[k : k + 1] for k in range(3)] + [ng_ref[...].reshape(1, D)]
+    halves = (0, 1, 5, 6)
     for k, column in enumerate(columns):
-        cols[k] = jnp.broadcast_to(column, (D, D)).T
+        cols[k] = jnp.broadcast_to(column * 0.5 if k in halves else column, (D, D)).T
+    table_t[:, FULL : FULL + NODES] = (
+        mm(halved(transposed(ew1_ref[2 * D : 3 * D])), full_t[:, 0:NODES]) + wide(cols[0], NODES)
+    ).astype(BF)
 
     def forward(i, carry):
         off = pl.multiple_of(i * CH, CH)
         at = pl.ds(off, CH)
         s_row = send_ref[0, 0, :, at]
         r_row = recv_ref[0, 0, :, at]
-        hot = one_hot_rows(s_row, SEND_TILES) + one_hot_rows(r_row, RECV_TILES)
-        rhs = jnp.concatenate(hot + [transposed(edge_ref[0, 0, 0, at])], 0)
-        p1 = mm(table_t[...], rhs) + wide(cols[0], CH)
+        to = jnp.concatenate(one_hot_rows(r_row, RECV_TILES), 0)
+        to_rows[i] = to
+        rhs = jnp.concatenate(one_hot_rows(s_row, SEND_TILES) + [to, transposed(edge_ref[0, 0, 0, at])], 0)
+        p1 = mm(table_t[...], rhs)
         a1, d1 = silu_parts(p1)
         b1 = a1.astype(BF)
         z1[i] = b1
@@ -313,9 +324,10 @@
         nrm[i] = n
         inv[i] = iv
         new = (n * wide(cols[3], CH) + wide(cols[4], CH)).astype(BF)
-        slo[at], shi[at], lo, hi = column_digits(s_row, r_row)
-        rlo[at], rhi[at] = lo, hi
-        part = mm(new, jnp.concatenate(one_hot_columns(lo, hi, RECV_TILES), 1))
+        slo[at], shi[at] = column_digits(s_row)
+        to = jnp.concatenate(one_hot_columns(*column_digits(r_row), RECV_TILES), 1)
+        to_cols[at] = to
+        part = mm(new, to)
 
         @pl.when(i == 0)
         def _():
@@ -332,17 +344,17 @@
     for cp in loads[14:]:
         cp.wait()
     node_in = jnp.concatenate([full_t[:, 0:NODES], agg[...].astype(BF)], 0)
-    a1, d1 = silu_parts(mm(transposed(nw1_ref[...]), node_in) + wide(cols[5], NODES))
+    a1, d1 = silu_parts(mm(halved(transposed(nw1_ref[...])), node_in) + wide(cols[5], NODES))
     b1 = a1.astype(BF)
-    a2, d2 = silu_parts(mm(transposed(nwh_ref[0]), b1) + wide(cols[6], NODES))
+    a2, d2 = silu_parts(mm(halved(transposed(nwh_ref[0])), b1) + wide(cols[6], NODES))
     b2 = a2.astype(BF)
     n, iv = norm_parts(mm(transposed(nwh_ref[1]), b2) + wide(cols[7], NODES))
     u = transposed(ncot_ref[0, 0, 0]).astype(F32)
     g3 = norm_back(u, wide(cols[8], NODES), n, iv)
     h3 = g3.astype(BF)
-    g2 = mm(nwh_ref[1], h3) * d2
+    g2 = mm(halved(nwh_ref[1]), h3) * d2
     h2 = g2.astype(BF)
-    g1 = mm(nwh_ref[0], h2) * d1
+    g1 = mm(halved(nwh_ref[0]), h2) * d1
     h1 = g1.astype(BF)
     node_h1[...] = h1
     aggb[...] = mm(nw1_ref[D : 2 * D], h1).astype(BF)
@@ -365,22 +377,24 @@
             else:
                 ref[where] += value
 
-        r_row = recv_ref[0, 0, :, at]
         cot = transposed(ecot_ref[0, 0, 0, at]).astype(F32)
-        u = cot + mm(aggb[...], jnp.concatenate(one_hot_rows(r_row, RECV_TILES), 0))
+        u = cot + mm(aggb[...], to_rows[i])
         n = nrm[i]
         g3 = norm_back(u, wide(cols[3], CH), n, inv[i])
         h3 = g3.astype(BF)
-        g2 = mm(ewh_ref[1], h3) * sl2[i]
+        g2 = mm(w3h[...], h3) * sl2[i]
         h2 = g2.astype(BF)
-        g1 = mm(ewh_ref[0], h2) * sl1[i]
+        g1 = mm(w2h[...], h2) * sl1[i]
         h1 = g1.astype(BF)
         g1b[i] = h1
-        add(pack_ref, pl.ds(ROW_EWH, D), mm_nt(z1[i], h2))
-        add(pack_ref, pl.ds(ROW_EWH + D, D), mm_nt(z2[i], h3))
-        hot = one_hot_columns(slo[at], shi[at], SEND_TILES) + one_hot_columns(rlo[at], rhi[at], RECV_TILES)
-        add(acc, slice(None), mm(h1, jnp.concatenate(hot + [edge_ref[0, 0, 0, at]], 1)))
-        for k, x in enumerate((g1, g2, g3, u * n, u)):
+        ones = jnp.ones((16, CH), BF)
+        for k, (z, h) in enumerate(((z1[i], h2), (z2[i], h3))):
+            grad = mm_nt(jnp.concatenate([z, ones], 0), h)
+            add(pack_ref, pl.ds(ROW_EWH + k * D, D), grad[0:D])
+            add(pack_ref, pl.ds(ROW_ESM + 1 + k, 1), grad[D : D + 1])
+        hot = one_hot_columns(slo[at], shi[at], SEND_TILES)
+        add(acc, slice(None), mm(h1, jnp.concatenate(hot + [to_cols[at], edge_ref[0, 0, 0, at]], 1)))
+        for k, x in enumerate((u * n, u)):
             add(small, k, fold(x))
 
     for i in range(CHUNKS):
@@ -394,11 +408,12 @@
     pack_ref[D : 2 * D] = mm_nt(full_t[...], sums) * edge_scale
     pack_ref[2 * D : 3 * D] = mm_nt(full_t[:, 0:NODES], sums_r) * edge_scale
     pack_ref[ROW_EWH : ROW_EWH + 2 * D] = pack_ref[ROW_EWH : ROW_EWH + 2 * D] * edge_scale
-    pack_ref[ROW_ESM : ROW_ESM + 5] = edge_scale * jnp.concatenate([lane_sum(small[j]) for j in range(5)], 0)
+    pack_ref[ROW_ESM + 1 : ROW_ESM + 3] = pack_ref[ROW_ESM + 1 : ROW_ESM + 3] * edge_scale
+    pack_ref[ROW_ESM : ROW_ESM + 1] = lane_sum(fold(acc[:, FULL : FULL + NODES])) * edge_scale
+    pack_ref[ROW_ESM + 3 : ROW_ESM + 5] = edge_scale * jnp.concatenate([lane_sum(small[0]), lane_sum(small[1])], 0)
     edge_reduce.swap_halves(pack_ref)
     back = mm_tn(sums, transposed(ew1_ref[D : 2 * D]))
     ghost_out_ref[...] = back[NODES:].reshape(FACES, SLOTS, D)
-    node_reduce.along_z()
     edge_reduce.in_plane()
     ghosts = send_ghosts(place, ghost_out_ref, gbuf, g_s, g_r)
     local_ref[...] = (
@@ -412,9 +427,10 @@
         edge_out_ref[0, 0, 0, at] = (
             ecot_ref[0, 0, 0, at].astype(F32) + mm_tn(g1b[i], transposed(ew1_ref[0:D]))
         ).astype(BF)
-    node_reduce.spread()
+    node_reduce.along_z()
     edge_reduce.along_z()
     node_out_ref[...] = add_ghosts(local_ref[...], ghosts, gbuf, rows_ref)
+    node_reduce.spread()
     edge_reduce.spread()
     node_reduce.swap_back()
     edge_reduce.swap_back()
@@ -442,14 +458,16 @@
         pltpu.VMEM((CHUNKS, 1, CH), F32),
         pltpu.VMEM((EDGES, D), BF),
         pltpu.VMEM((EDGES, D), BF),
-        pltpu.VMEM((EDGES, D), BF),
-        pltpu.VMEM((EDGES, D), BF),
+        pltpu.VMEM((CHUNKS, NODES, CH), BF),
+        pltpu.VMEM((EDGES, NODES), BF),
         pltpu.VMEM((CHUNKS, D, CH), BF),
         pltpu.VMEM((D, NODES), F32),
         pltpu.VMEM((D, FULL + NODES + D), F32),
         pltpu.VMEM((D, NODES), BF),
-        pltpu.VMEM((5, D, D), F32),
+        pltpu.VMEM((2, D, D), F32),
         pltpu.VMEM((9, D, D), F32),
+        pltpu.VMEM((D, D), BF),
+        pltpu.VMEM((D, D), BF),
         pltpu.VMEM((D, D), BF),
         pltpu.VMEM((D, D), BF),
         pltpu.VMEM((D, NODES), BF),

time: 42.4 us -> 40.2 us (0.948)
  Pallas kernels: 41.7 us -> 39.5 us
    pallas_call x1, Pallas kernels: 40.4 us -> 38.2 us  [fused(): pl.pallas_call(functools.partial(fused_kernel, scales), out_shape=(jax.Sh...]
where the time goes in v5:
time: 40.2 us; the launch traced here: 40.1 us
  Pallas kernels  39.5 us (98%)
  between operations  0.66 us (2%)
    pallas_call x1, Pallas kernels, fused(): pl.pallas_call(functools.partial(fused_kernel, scales), out_shape=(jax.Sh...  38.2 us
    pallas_call x1, Pallas kernels, unpack(): pl.pallas_call(unpack_kernel, out_shape=(jax.ShapeDtypeStruct(edge.shape,...  1.25 us

profile of v5, /device:TPU:1, one launch (start us, length us, event | category | flops | bytes accessed | tf_op | source)
XLA Modules:
  0.0 40.1 jit_solution(15315070545867681591)
XLA Ops:
  0.7 38.2 %shard_map.248 = (bf16[1,1,1,2816,128]{4,3,2,1,0:T(8,128)(2,1)S(1)}, f32[672,128]{1,0:T(8,128)S(1)}, f32[544,128]{1,0:T(8,128)S(1)}, f32[512,128]{1,0:T(8,128)S(1)}) custom-call(bf16[1,1,1,512,128]{4,3,2,1,0:T(8,128)(2,1)} %refs_0_.1, bf16[1,1,1,6,64,128]{5,4,3,2,1,0:T(8,128)(2,1)} %refs_1_.1, bf16[384,128]{1,0:T(8,128)(2,1)} %refs_2_.1, ...), custom_call_target="tpu_custom_call" | custom-call | flops 6000000000 | bytes 6000000 | tf_op jit(solution)/shard_map/pallas_call | solution.py:487
  38.9 1.3 %shard_map.249 = (bf16[1,1,1,2816,128]{4,3,2,1,0:T(8,128)(2,1)}, f32[1,1,1,512,128]{4,3,2,1,0:T(8,128)}, f32[384,128]{1,0:T(8,128)}, f32[2,128,128]{2,1,0:T(8,12...) custom-call(bf16[1,1,1,2816,128]{4,3,2,1,0:T(8,128)(2,1)S(1)} %get-t, ...), custom_call_target="tpu_custom_call" | custom-call | flops 1000000 | bytes 4000000 | tf_op jit(solution)/shard_map/pallas_call | solution.py:537

commit v6 on v5

--- a/solution.py
+++ b/solution.py
@@ -17,7 +17,7 @@
 SLOTS = 64
 FULL = NODES + FACES * SLOTS
 EDGES = 2816
-CH = 1408
+CH = 2816
 CHUNKS = EDGES // CH
 SEND_TILES = FULL // D
 RECV_TILES = NODES // D
@@ -163,9 +163,10 @@
         self.started.append(cp)
         return cp
 
-    def drain(self):
-        for cp in self.started:
+    def drain(self, count):
+        for cp in self.started[:count]:
             cp.wait_send()
+        self.started = self.started[count:]
 
 
 class AllReduce:
@@ -301,9 +302,8 @@
         mm(halved(transposed(ew1_ref[2 * D : 3 * D])), full_t[:, 0:NODES]) + wide(cols[0], NODES)
     ).astype(BF)
 
-    def forward(i, carry):
-        off = pl.multiple_of(i * CH, CH)
-        at = pl.ds(off, CH)
+    def forward(i):
+        at = pl.ds(i * CH, CH)
         s_row = send_ref[0, 0, :, at]
         r_row = recv_ref[0, 0, :, at]
         to = jnp.concatenate(one_hot_rows(r_row, RECV_TILES), 0)
@@ -329,17 +329,13 @@
         to_cols[at] = to
         part = mm(new, to)
 
-        @pl.when(i == 0)
-        def _():
+        if i == 0:
             agg[...] = part
-
-        @pl.when(i > 0)
-        def _():
+        else:
             agg[...] += part
 
-        return carry
-
-    lax.fori_loop(0, CHUNKS, forward, 0)
+    for i in range(CHUNKS):
+        forward(i)
 
     for cp in loads[14:]:
         cp.wait()
@@ -364,8 +360,6 @@
     node_pack_ref[ROW_NSM : ROW_NSM + 4] = node_scale * jnp.concatenate(
         [lane_sum(fold(g1)), lane_sum(fold(g2)), lane_sum(fold(g3)), lane_sum(fold(u * n))], 0
     )
-    place.meet()
-    node_reduce.swap_halves(node_pack_ref)
 
     def backward(i):
         at = pl.ds(i * CH, CH)
@@ -387,6 +381,9 @@
         g1 = mm(w2h[...], h2) * sl1[i]
         h1 = g1.astype(BF)
         g1b[i] = h1
+        if i == 0:
+            place.meet()
+            node_reduce.swap_halves(node_pack_ref)
         ones = jnp.ones((16, CH), BF)
         for k, (z, h) in enumerate(((z1[i], h2), (z2[i], h3))):
             grad = mm_nt(jnp.concatenate([z, ones], 0), h)
@@ -431,12 +428,14 @@
     edge_reduce.along_z()
     node_out_ref[...] = add_ghosts(local_ref[...], ghosts, gbuf, rows_ref)
     node_reduce.spread()
+    sent = len(place.started)
     edge_reduce.spread()
     node_reduce.swap_back()
+    place.drain(sent)
     edge_reduce.swap_back()
     node_reduce.finish(node_sum_ref)
+    place.drain(len(place.started))
     edge_reduce.finish(edge_sum_ref)
-    place.drain()
 
 
 VMEM = pl.BlockSpec(memory_space=pltpu.VMEM)

time: 40.2 us -> 38.2 us (0.950)
  Pallas kernels: 39.5 us -> 37.4 us
    pallas_call x1, Pallas kernels: 38.2 us -> 36.2 us  [fused(): pl.pallas_call(functools.partial(fused_kernel, scales), out_shape=(jax.Sh...]
where the time goes in v6:
time: 38.2 us; the launch traced here: 38.1 us
  Pallas kernels  37.4 us (98%)
  between operations  0.66 us (2%)
    pallas_call x1, Pallas kernels, fused(): pl.pallas_call(functools.partial(fused_kernel, scales), out_shape=(jax.Sh...  36.2 us
    pallas_call x1, Pallas kernels, unpack(): pl.pallas_call(unpack_kernel, out_shape=(jax.ShapeDtypeStruct(edge.shape,...  1.25 us

profile of v6, /device:TPU:1, one launch (start us, length us, event | category | flops | bytes accessed | tf_op | source)
XLA Modules:
  0.0 38.1 jit_solution(3976682302220866526)
XLA Ops:
  0.7 36.2 %shard_map.248 = (bf16[1,1,1,2816,128]{4,3,2,1,0:T(8,128)(2,1)S(1)}, f32[672,128]{1,0:T(8,128)S(1)}, f32[544,128]{1,0:T(8,128)S(1)}, f32[512,128]{1,0:T(8,128)S(1)}) custom-call(bf16[1,1,1,512,128]{4,3,2,1,0:T(8,128)(2,1)} %refs_0_.1, bf16[1,1,1,6,64,128]{5,4,3,2,1,0:T(8,128)(2,1)} %refs_1_.1, bf16[384,128]{1,0:T(8,128)(2,1)} %refs_2_.1, ...), custom_call_target="tpu_custom_call" | custom-call | flops 6000000000 | bytes 6000000 | tf_op jit(solution)/shard_map/pallas_call | solution.py:486
  36.8 1.3 %shard_map.249 = (bf16[1,1,1,2816,128]{4,3,2,1,0:T(8,128)(2,1)}, f32[1,1,1,512,128]{4,3,2,1,0:T(8,128)}, f32[384,128]{1,0:T(8,128)}, f32[2,128,128]{2,1,0:T(8,12...) custom-call(bf16[1,1,1,2816,128]{4,3,2,1,0:T(8,128)(2,1)S(1)} %get-t, ...), custom_call_target="tpu_custom_call" | custom-call | flops 1000000 | bytes 4000000 | tf_op jit(solution)/shard_map/pallas_call | solution.py:536

commit v7 on v6

--- a/solution.py
+++ b/solution.py
@@ -117,6 +117,17 @@
     return [jnp.where(hi == BF(k), base, zero) for k in range(tiles)]
 
 
+class Bytes:
+    def __init__(self, ref, sem):
+        self.copy = pltpu.make_async_copy(ref, ref, sem)
+
+    def wait_recv(self):
+        self.copy.wait()
+
+    def wait_send(self):
+        self.copy.wait()
+
+
 class Place:
     def __init__(self):
         gx, gy, gz = lax.axis_index("gx"), lax.axis_index("gy"), lax.axis_index("gz")
@@ -155,13 +166,17 @@
     def meet(self):
         pl.semaphore_wait(pltpu.get_barrier_semaphore(), self.greeted)
 
-    def remote(self, src, dst, send, recv, peer):
+    def remote(self, src, dst, send, recv, peer, keep=True):
         cp = pltpu.make_async_remote_copy(
             src_ref=src, dst_ref=dst, send_sem=send, recv_sem=recv, device_id=peer, device_id_type=MESH
         )
         cp.start()
-        self.started.append(cp)
+        if keep:
+            self.started.append(cp)
         return cp
+
+    def sent(self, ref, sem):
+        self.started.append(Bytes(ref, sem))
 
     def drain(self, count):
         for cp in self.started[:count]:
@@ -193,12 +208,11 @@
         place = self.place
         self.arrived()
         self.half[...] = self.src[pl.ds(place.c * 16, 16)] + self.pair[...]
-        self.pending = []
         for d in PLANE_ORDER:
             index, peer = place.plane_peer(d)
-            self.pending.append(
-                place.remote(self.half.at[index], self.inbox.at[d], self.rs_s.at[d], self.rs_r.at[d], peer)
-            )
+            place.remote(self.half.at[index], self.inbox.at[d], self.rs_s.at[0], self.rs_r.at[0], peer, keep=False)
+        place.sent(self.half.at[0:15], self.rs_s.at[0])
+        self.pending = [Bytes(self.inbox.at[1:16], self.rs_r.at[0])]
 
     def along_z(self):
         self.arrived()
@@ -208,9 +222,10 @@
         z = self.place.z
         self.zbuf[z] = own
         piece = self.zbuf.at[z]
-        self.pending = [
-            self.place.remote(piece, piece, self.z_s.at[d], self.z_r.at[d], self.place.z_peer(d)) for d in Z_ORDER
-        ]
+        for d in Z_ORDER:
+            self.place.remote(piece, piece, self.z_s.at[0], self.z_r.at[0], self.place.z_peer(d), keep=False)
+        self.place.sent(self.zbuf.at[0:7], self.z_s.at[0])
+        self.pending = [Bytes(self.zbuf.at[0:7], self.z_r.at[0])]
 
     def spread(self):
         place = self.place
@@ -222,9 +237,11 @@
         self.fin[mine] = own
         piece = self.fin.at[mine]
         self.pending = [
-            place.remote(piece, piece, self.ag_s.at[d], self.ag_r.at[d], place.plane_peer(d)[1]) for d in PLANE_ORDER
+            place.remote(piece, piece, self.ag_s.at[0], self.ag_r.at[d], place.plane_peer(d)[1], keep=False)
+            for d in PLANE_ORDER
         ]
-        self.backs = [place.remote(piece, piece, self.back_s.at[0], self.back_r.at[0], place.sibling)]
+        place.sent(self.fin.at[0:15], self.ag_s.at[0])
+        place.remote(piece, piece, self.back_s.at[0], self.back_r.at[0], place.sibling, keep=False)
 
     def swap_back(self):
         place = self.place
@@ -232,8 +249,9 @@
             cp.wait_recv()
             source = (4 - d // 4) % 4 * 4 + (4 - d % 4) % 4
             piece = self.fin.at[place.c * 16 + place.plane_peer(source)[0]]
-            self.backs.append(place.remote(piece, piece, self.back_s.at[d], self.back_r.at[d], place.sibling))
-        self.pending = self.backs
+            place.remote(piece, piece, self.back_s.at[0], self.back_r.at[0], place.sibling, keep=False)
+        place.sent(self.fin.at[0:16], self.back_s.at[0])
+        self.pending = [Bytes(self.fin.at[0:16], self.back_r.at[0])]
 
     def finish(self, out_ref):
         self.arrived()
@@ -477,7 +495,7 @@
     ]
     for piece in (EDGE_PIECE, NODE_PIECE):
         scratch += [pltpu.VMEM((n, piece, D), F32) for n in (PIECES, 16, 16, 16, 8, PIECES)]
-        scratch += [pltpu.SemaphoreType.DMA((n,)) for n in (1, 1, 16, 16, 8, 8, 16, 16, 16, 16)]
+        scratch += [pltpu.SemaphoreType.DMA((n,)) for n in (1, 1, 1, 1, 1, 1, 1, 16, 1, 1)]
     scratch += [
         pltpu.VMEM((FACES, SLOTS, D), F32),
         pltpu.SemaphoreType.DMA((FACES,)),

time: 38.2 us -> 36.6 us (0.958)
  Pallas kernels: 37.4 us -> 35.8 us
    pallas_call x1, Pallas kernels: 36.2 us -> 34.6 us  [fused(): pl.pallas_call(functools.partial(fused_kernel, scales), out_shape=(jax.Sh...]
where the time goes in v7:
time: 36.6 us; the launch traced here: 36.5 us
  Pallas kernels  35.8 us (98%)
  between operations  0.66 us (2%)
    pallas_call x1, Pallas kernels, fused(): pl.pallas_call(functools.partial(fused_kernel, scales), out_shape=(jax.Sh...  34.6 us
    pallas_call x1, Pallas kernels, unpack(): pl.pallas_call(unpack_kernel, out_shape=(jax.ShapeDtypeStruct(edge.shape,...  1.25 us

profile of v7, /device:TPU:1, one launch (start us, length us, event | category | flops | bytes accessed | tf_op | source)
XLA Modules:
  0.0 36.5 jit_solution(8810127938312997628)
XLA Ops:
  0.7 34.6 %shard_map.248 = (bf16[1,1,1,2816,128]{4,3,2,1,0:T(8,128)(2,1)S(1)}, f32[672,128]{1,0:T(8,128)S(1)}, f32[544,128]{1,0:T(8,128)S(1)}, f32[512,128]{1,0:T(8,128)S(1)}) custom-call(bf16[1,1,1,512,128]{4,3,2,1,0:T(8,128)(2,1)} %refs_0_.1, bf16[1,1,1,6,64,128]{5,4,3,2,1,0:T(8,128)(2,1)} %refs_1_.1, bf16[384,128]{1,0:T(8,128)(2,1)} %refs_2_.1, ...), custom_call_target="tpu_custom_call" | custom-call | flops 6000000000 | bytes 6000000 | tf_op jit(solution)/shard_map/pallas_call | solution.py:504
  35.2 1.3 %shard_map.249 = (bf16[1,1,1,2816,128]{4,3,2,1,0:T(8,128)(2,1)}, f32[1,1,1,512,128]{4,3,2,1,0:T(8,128)}, f32[384,128]{1,0:T(8,128)}, f32[2,128,128]{2,1,0:T(8,12...) custom-call(bf16[1,1,1,2816,128]{4,3,2,1,0:T(8,128)(2,1)S(1)} %get-t, ...), custom_call_target="tpu_custom_call" | custom-call | flops 1000000 | bytes 4000000 | tf_op jit(solution)/shard_map/pallas_call | solution.py:554
